TPU v7x, 512 devices: a whole 4x8x8 slice. The times are simulated.
512 devices in a mesh: seq: 32 (over z, x), mp: 16 (over y, core).
Axes of the slice: x: 4, y: 8, z: 8, core: 2. Of those that a mesh axis runs over, the one named last changes fastest.
Arguments:
- inputs: bfloat16 [16384, 4096], P('seq', 'mp'), may hold values from -6 to 6
- guess: float32 [16384, 2, 2048], P('seq', None, 'mp'), may hold values from -4 to 4
- initial: float32 [2, 2048], P(None, 'mp'), may hold values from -4 to 4
- w_in: bfloat16 [4096, 2, 2048], P(None, None, 'mp'), may hold values from -0.09375 to 0.09375
- bias: float32 [2, 2048], P(None, 'mp'), may hold values from -3 to 3
- angle: float32 [2048], P('mp'), may hold values from -3.140625 to 3.140625
- strength: float32 [2048], P('mp'), may hold values from 0 to 1, as said below
- w_out: bfloat16 [2, 2048, 4096], P(None, 'mp'), may hold values from -0.09375 to 0.09375
Outputs:
- new_state: float32 [16384, 2, 2048], P('seq', None, 'mp')
- output: bfloat16 [16384, 4096], P('seq', 'mp')
Inputs may be any that keep to these rules, and one draw needn't show every extreme that they name: `strength`: each pair's nonlinear weight; every value lies either between 0.3 and 1 (strongly nonlinear pairs) or between 0.1 / 16384 and 1 / 16384 (pairs nearly linear over the whole sequence), in any mix.
All inputs are finite; a program needn't handle non-finite values.
Results may differ from a plain program's by a relative error of at most 0.018.
Values may be sent and summed in bfloat16 or wider, within the bound.
A program may use at most 64 MiB of HBM per device.

v0:
```python
import jax
import jax.numpy as jnp
from jax import lax
from jax.sharding import Mesh
from jax.sharding import PartitionSpec as P

MP = ("mp_0", "mp_1")


def shifted(value, axis, steps):
    count = lax.axis_size(axis)
    first, last = (max(0, -steps), min(count, count - steps))
    return lax.ppermute(value, axis, [(source, source + steps) for source in range(first, last)])


def copy_for_each(shard, axis):
    size = lax.axis_size(axis)
    return lax.all_to_all(
        jnp.broadcast_to(shard[None], (size, *shard.shape)), axis, 0, 0, tiled=True
    )


def collected_together(shard, axis):
    leaves = jax.tree.leaves(shard)
    order = sorted(range(len(leaves)), key=lambda k: -leaves[k].size)
    width = (1, *leaves[order[0]].shape)[-1]
    lines = [
        jnp.pad(leaves[k].reshape(-1), (0, -leaves[k].size % width)).reshape(-1, width)
        for k in order
    ]
    both, at, found = (copy_for_each(jnp.concatenate(lines), axis), 0, {})
    for k, line in zip(order, lines):
        section = both[:, at : at + len(line)].reshape(len(both), -1)
        found[k] = section[:, : leaves[k].size].reshape(-1, *leaves[k].shape)
        at += len(line)
    numbers = iter(range(len(leaves)))
    return jax.tree.map(lambda _: found[next(numbers)], shard)


def joined_by_halves(pieces, combine):
    while len(jax.tree.leaves(pieces)[0]) > 1:
        pieces = jax.vmap(combine)(
            *(jax.tree.map(lambda part: part[side::2], pieces) for side in (0, 1))
        )
    return jax.tree.map(lambda part: part[0], pieces)


def prefix(shard, axis, combine, identity):
    size, position = (lax.axis_size(axis), lax.axis_index(axis))
    passed = jnp.arange(size) < position

    def kept(part, zero, own):
        part = jnp.where(
            passed.reshape(-1, *(1 for _ in own.shape)), part, jnp.asarray(zero, own.dtype)
        )
        return part

    pieces = collected_together(shard, axis)
    return joined_by_halves(jax.tree.map(kept, pieces, identity, shard), combine)


def cut_along(shard, dim, size):
    lengths = shard.shape
    tiles = shard.reshape(*lengths[:dim], size, lengths[dim] // size, *lengths[dim + 1 :])
    return jnp.moveaxis(tiles, dim, 0)


def sum_at_owner(shard, axis, dim):
    size = lax.axis_size(axis)
    tiles = lax.all_to_all(cut_along(shard, dim, size), axis, 0, 0, tiled=True)
    return jnp.sum(tiles.astype(jnp.float32), axis=0)


def sum_in_two_steps(shard, axes, dim):
    far, near = axes
    own = sum_at_owner(cut_along(shard, dim, lax.axis_size(far)), near, dim + 1)
    return jnp.sum(
        lax.all_to_all(own.astype(jnp.bfloat16), far, 0, 0, tiled=True).astype(jnp.float32), axis=0
    )


def linearize(previous, drive, angle, strength):
    cosine = jnp.cos(angle)
    sine = jnp.sin(angle)
    first = cosine * previous[:, 0] - sine * previous[:, 1]
    second = sine * previous[:, 0] + cosine * previous[:, 1]
    squash_one = jnp.tanh(first + drive[:, 0])
    squash_two = jnp.tanh(second + drive[:, 1])
    value_one = first + strength * (squash_one - first)
    value_two = second + strength * (squash_two - second)
    slope_one = 1.0 - strength * squash_one * squash_one
    slope_two = 1.0 - strength * squash_two * squash_two
    jac_aa = slope_one * cosine
    jac_ab = -slope_one * sine
    jac_ba = slope_two * sine
    jac_bb = slope_two * cosine
    offset_one = value_one - (jac_aa * previous[:, 0] + jac_ab * previous[:, 1])
    offset_two = value_two - (jac_ba * previous[:, 0] + jac_bb * previous[:, 1])
    return (jac_aa, jac_ab, jac_ba, jac_bb, offset_one, offset_two)


def compose(earlier, later):
    lat_aa, lat_ab, lat_ba, lat_bb, lat_one, lat_two = later
    ear_aa, ear_ab, ear_ba, ear_bb, ear_one, ear_two = earlier
    return (
        lat_aa * ear_aa + lat_ab * ear_ba,
        lat_aa * ear_ab + lat_ab * ear_bb,
        lat_ba * ear_aa + lat_bb * ear_ba,
        lat_ba * ear_ab + lat_bb * ear_bb,
        lat_aa * ear_one + lat_ab * ear_two + lat_one,
        lat_ba * ear_one + lat_bb * ear_two + lat_two,
    )


def apply_map(mapping, state):
    map_aa, map_ab, map_ba, map_bb, map_one, map_two = mapping
    first = map_aa * state[0] + map_ab * state[1] + map_one
    second = map_ba * state[0] + map_bb * state[1] + map_two
    return jnp.stack([first, second])


def local(inputs, guess, initial, w_in, bias, angle, strength, w_out):
    local_steps = inputs.shape[0]
    local_pairs = initial.shape[1]
    width = w_in.shape[0]
    w_flat = w_in.reshape(width, 2 * local_pairs)
    drive = jnp.dot(
        lax.all_gather(inputs, MP, axis=1, tiled=True), w_flat, preferred_element_type=jnp.float32
    )
    drive = drive.reshape(local_steps, 2, local_pairs) + bias[None]
    position = lax.axis_index("seq")
    arrived = shifted(guess[-1], "seq", 1)
    entering_guess = jnp.where(position == 0, initial, arrived)
    previous = jnp.concatenate([entering_guess[None], guess[:-1]], axis=0)
    terms = linearize(previous, drive, angle, strength)
    cumulative = lax.associative_scan(compose, terms, axis=0)
    totals = tuple((member[-1] for member in cumulative))
    ones = jnp.ones((local_pairs,), jnp.float32)
    zeros = jnp.zeros((local_pairs,), jnp.float32)
    identity = (ones, zeros, zeros, ones, zeros, zeros)
    before = prefix(totals, "seq", compose, identity)
    entering = apply_map(before, initial)
    cum_aa, cum_ab, cum_ba, cum_bb, cum_one, cum_two = cumulative
    first = cum_aa * entering[0][None] + cum_ab * entering[1][None] + cum_one
    second = cum_ba * entering[0][None] + cum_bb * entering[1][None] + cum_two
    new_state = jnp.stack([first, second], axis=1)
    flat_state = new_state.astype(jnp.bfloat16).reshape(local_steps, 2 * local_pairs)
    terms_out = jnp.dot(
        flat_state, w_out.reshape(2 * local_pairs, width), preferred_element_type=jnp.float32
    )
    output = sum_in_two_steps(terms_out.astype(jnp.bfloat16), ("mp_0", "mp_1"), 1).astype(
        jnp.bfloat16
    )
    return (new_state, output)


def solution(mesh):
    torus = Mesh(mesh.devices.reshape(mesh.shape["seq"], 8, 2), ("seq", "mp_0", "mp_1"))
    placed = (
        P("seq", MP),
        P("seq", None, MP),
        P(None, MP),
        P(None, None, MP),
        P(None, MP),
        P(MP),
        P(MP),
        P(None, MP, None),
    )
    return jax.shard_map(
        local,
        mesh=torus,
        in_specs=placed,
        out_specs=(P("seq", None, MP), P("seq", MP)),
        check_vma=False,
    )
```

profile of v0, /device:TPU:8, one launch (start us, length us, event | category | flops | bytes accessed | tf_op | source)
XLA Modules:
  0.0 309.7 jit_solution(3582479941553940593)
XLA Ops:
  8.6 3.4 %collective-permute-start = (f32[2,128]{1,0:T(2,128)S(1)}, f32[2,128]{1,0:T(2,128)S(1)}, u32[]{:S(2)}, u32[]{:S(2)}) collective-permute-start(f32[2,128]{1,0:T(2,128)S(1)} %slice_bitcast_fusion.2), channel_id=1, source_target_pairs={{0,16},{16,32},{32,48},{48,64},{64,80},{80,96},{96,112},{112,128},... | collective-permute-start | bytes 3080 | tf_op jit(solution)/shard_map/ppermute | solution.py:13
  13.8 3.3 %copy.55 = bf16[512,8,2,128]{3,1,2,0:T(8,128)(2,1)} copy(bf16[512,8,2,128]{3,2,1,0:T(2,128)(2,1)} %bitcast.83) | data formatting | bytes 4194304
  17.1 4.2 %copy.34 = bf16[256,4096]{1,0:T(8,128)(2,1)} copy(bf16[256,4096]{0,1:T(8,128)(2,1)} %bitcast.82) | data formatting | bytes 4194304 | tf_op jit(solution)/shard_map/dot_general | solution.py:127
  21.3 44.4 %all-gather.2.cloned.1.call-done = bf16[512,4096]{1,0:T(8,128)(2,1)} async-done(((bf16[512,256]{1,0:T(8,128)(2,1)}), bf16[512,4096]{1,0:T(8,128)(2,1)}) %all-gather.2.cloned.1.call-update) | async-done | bytes 4194320 | tf_op jit(solution)/shard_map/all_gather | solution.py:128
  65.7 4.2 %fusion.2 = f32[512,2,128]{2,0,1:T(8,128)S(1)} fusion(bf16[2,128,4096]{2,1,0:T(8,128)(2,1)} %bitcast.84, bf16[512,4096]{1,0:T(8,128)(2,1)} %all-gather.2.cloned.1.call-done, f32[2,128]{1,0:T(2,128)S(1)} %copy-done.47), kind=kOutput, calls=%fused_computation.4 | convolution fusion | flops 1073872896 | bytes 6816768 | tf_op jit(solution)/shard_map/dot_general | solution.py:127
  79.1 1.6 slice.1056
  80.7 1.6 slice.1049
  82.3 1.6 slice.1060
  83.9 1.6 slice.1057
  135.9 1.6 add.1065
  138.1 1.7 multiply_add_fusion.3
  156.2 1.7 pad_maximum_fusion.5
  158.9 1.7 pad_maximum_fusion.4
  160.5 2.4 pad.398
  164.5 2.3 pad.362
  166.8 1.6 pad_maximum_fusion.3
  168.4 2.3 pad.396
  170.7 2.3 pad.363
  173.1 2.3 pad.397
  175.4 2.4 pad.401
  182.8 10.4 %all-to-all-start = ((f32[32,6,128]{2,1,0:T(8,128)}), f32[32,6,128]{2,1,0:T(8,128)S(1)}, u32[]{:S(2)}, u32[]{:S(2)}) async-start(f32[32,6,128]{2,1,0:T(8,128)} %broadcast_in_dim.60), calls=%async_computation | async-start | bytes 262144 | tf_op jit(solution)/shard_map/all_to_all | solution.py:18
  193.1 10.7 %all-to-all-done = f32[32,6,128]{2,1,0:T(8,128)S(1)} async-done(((f32[32,6,128]{2,1,0:T(8,128)}), f32[32,6,128]{2,1,0:T(8,128)S(1)}, u32[]{:S(2)}, u32[]{:S(2)}) %all-to-all-start) | async-done | bytes 98336 | tf_op jit(solution)/shard_map/all_to_all | solution.py:18
  204.9 1.7 add_bitcast_fusion.1
  206.6 3.3 %bitcast_convert_fusion = bf16[512,4096]{1,0:T(8,128)(2,1)} fusion(bf16[2,128,4096]{2,1,0:T(8,128)(2,1)S(1)} %copy-done, f32[512,1,128]{2,0,1:T(8,128)S(1)} %get-tuple-element.159, f32[512,1,128]{2,0,1:T(8,128)S(1)} %get-tuple-element.158), kind=kOutput, calls=%fused_computation | convolution fusion | flops 1075970048 | bytes 6815744 | tf_op jit(solution)/shard_map/dot_general | solution.py:148
  209.9 6.5 %copy.45 = bf16[512,4096]{0,1:T(8,128)(2,1)} copy(bf16[512,4096]{1,0:T(8,128)(2,1)} %bitcast_convert_fusion) | data formatting | bytes 8388608 | tf_op jit(solution)/shard_map/reshape | solution.py:64
  216.4 8.0 %copy.41 = bf16[2,8,512,256]{3,1,2,0:T(8,128)(2,1)} copy(bf16[2,8,512,256]{2,3,0,1:T(8,128)(2,1)} %bitcast.81) | data formatting | bytes 8388608 | tf_op jit(solution)/shard_map/transpose | solution.py:65
  224.4 11.8 %all_to_all.15 = bf16[2,8,512,256]{3,1,2,0:T(8,128)(2,1)} all-to-all(bf16[2,8,512,256]{3,1,2,0:T(8,128)(2,1)} %copy.41), channel_id=1, replica_groups=mesh['seq'=32,'mp_0'=8,'mp_1'=2] {'mp_1'}, dimensions={0} | all-to-all | bytes 8388608 | tf_op jit(solution)/shard_map/all_to_all | solution.py:70
  236.2 4.9 %reduce_sum.24 = bf16[8,512,256]{2,0,1:T(8,128)(2,1)} reduce(bf16[2,8,512,256]{3,1,2,0:T(8,128)(2,1)} %all_to_all.15, bf16[]{:T(256)} %constant.16.clone.1), dimensions={0}, to_apply=%region_0.1 | reduce | flops 1048576 | bytes 6291458 | tf_op jit(solution)/shard_map/reduce_sum | solution.py:71
  241.2 3.3 %copy.43 = bf16[8,512,256]{2,1,0:T(8,128)(2,1)} copy(bf16[8,512,256]{2,0,1:T(8,128)(2,1)} %reduce_sum.24) | data formatting | bytes 4194304 | tf_op jit(solution)/shard_map/reduce_sum | solution.py:71
  244.5 5.4 %all-to-all-start.2 = ((bf16[8,512,256]{2,1,0:T(8,128)(2,1)}), bf16[8,512,256]{2,1,0:T(8,128)(2,1)}, u32[]{:S(2)}, u32[]{:S(2)}) async-start(bf16[8,512,256]{2,1,0:T(8,128)(2,1)} %copy.43), calls=%async_computation.2 | async-start | bytes 4194304 | tf_op jit(solution)/shard_map/all_to_all | solution.py:78
  251.1 49.2 %all-to-all-done.2 = bf16[8,512,256]{2,1,0:T(8,128)(2,1)} async-done(((bf16[8,512,256]{2,1,0:T(8,128)(2,1)}), bf16[8,512,256]{2,1,0:T(8,128)(2,1)}, u32[]{:S(2)}, u32[]{:S(2)}) %all-to-all-start.2) | async-done | bytes 2097184 | tf_op jit(solution)/shard_map/all_to_all | solution.py:78
  300.3 2.6 reduce_sum.25
  (556 shorter events, 88.0 us)
Async XLA Ops:
  7.2 199.5 %copy-start = (bf16[2,128,4096]{2,1,0:T(8,128)(2,1)S(1)}, bf16[2,128,4096]{2,1,0:T(8,128)(2,1)}, u32[]{:S(2)}) copy-start(bf16[2,128,4096]{2,1,0:T(8,128)(2,1)} %param.15) | copy-start | bytes 6291460
  7.2 58.5 %all-gather.2.cloned.1.call-start = ((), (), s32[]{:S(2)}) async-start(), calls=%async_computation.3 | async-start | bytes 4456448 | tf_op jit(solution)/shard_map/all_gather | solution.py:128
  8.6 12.7 %collective-permute-start = (f32[2,128]{1,0:T(2,128)S(1)}, f32[2,128]{1,0:T(2,128)S(1)}, u32[]{:S(2)}, u32[]{:S(2)}) collective-permute-start(f32[2,128]{1,0:T(2,128)S(1)} %slice_bitcast_fusion.2), channel_id=1, source_target_pairs={{0,16},{16,32},{32,48},{48,64},{64,80},{80,96},{96,112},{112,128},... | collective-permute-start | bytes 3080 | tf_op jit(solution)/shard_map/ppermute | solution.py:13
  17.1 48.6 %copy-start.47 = (f32[2,128]{1,0:T(2,128)S(1)}, f32[2,128]{1,0:T(2,128)}, u32[]{:S(2)}) copy-start(f32[2,128]{1,0:T(2,128)} %param.12) | copy-start | bytes 3076
  94.5 35.8 %copy-start.4 = (f32[127,128]{1,0:T(8,128)}, f32[127,128]{1,0:T(8,128)S(1)}, u32[]{:S(2)}) copy-start(f32[127,128]{1,0:T(8,128)S(1)} %slice.1174) | copy-start | bytes 195076
  95.1 35.2 %copy-start.6 = (f32[127,128]{1,0:T(8,128)}, f32[127,128]{1,0:T(8,128)S(1)}, u32[]{:S(2)}) copy-start(f32[127,128]{1,0:T(8,128)S(1)} %slice.1053) | copy-start | bytes 195076
  95.7 34.6 %copy-start.8 = (f32[127,128]{1,0:T(8,128)}, f32[127,128]{1,0:T(8,128)S(1)}, u32[]{:S(2)}) copy-start(f32[127,128]{1,0:T(8,128)S(1)} %slice.1166) | copy-start | bytes 195076
  96.2 34.1 %copy-start.10 = (f32[127,128]{1,0:T(8,128)}, f32[127,128]{1,0:T(8,128)S(1)}, u32[]{:S(2)}) copy-start(f32[127,128]{1,0:T(8,128)S(1)} %slice.1175) | copy-start | bytes 195076
  108.6 19.5 %copy-start.15 = (f32[63,128]{1,0:T(8,128)}, f32[63,128]{1,0:T(8,128)S(1)}, u32[]{:S(2)}) copy-start(f32[63,128]{1,0:T(8,128)S(1)} %slice.1168) | copy-start | bytes 96772
  109.2 18.8 %copy-start.17 = (f32[63,128]{1,0:T(8,128)}, f32[63,128]{1,0:T(8,128)S(1)}, u32[]{:S(2)}) copy-start(f32[63,128]{1,0:T(8,128)S(1)} %slice.1063) | copy-start | bytes 96772
  109.8 18.2 %copy-start.19 = (f32[63,128]{1,0:T(8,128)}, f32[63,128]{1,0:T(8,128)S(1)}, u32[]{:S(2)}) copy-start(f32[63,128]{1,0:T(8,128)S(1)} %slice.1160) | copy-start | bytes 96772
  110.4 17.7 %copy-start.21 = (f32[63,128]{1,0:T(8,128)}, f32[63,128]{1,0:T(8,128)S(1)}, u32[]{:S(2)}) copy-start(f32[63,128]{1,0:T(8,128)S(1)} %slice.1169) | copy-start | bytes 96772
  116.3 11.5 %copy-start.27 = (f32[31,128]{1,0:T(8,128)}, f32[31,128]{1,0:T(8,128)S(1)}, u32[]{:S(2)}) copy-start(f32[31,128]{1,0:T(8,128)S(1)} %slice.1073) | copy-start | bytes 47620
  116.3 11.5 %copy-start.28 = (f32[31,128]{1,0:T(8,128)}, f32[31,128]{1,0:T(8,128)S(1)}, u32[]{:S(2)}) copy-start(f32[31,128]{1,0:T(8,128)S(1)} %slice.1154) | copy-start | bytes 47620
  116.4 11.4 %copy-start.29 = (f32[31,128]{1,0:T(8,128)}, f32[31,128]{1,0:T(8,128)S(1)}, u32[]{:S(2)}) copy-start(f32[31,128]{1,0:T(8,128)S(1)} %slice.1163) | copy-start | bytes 47620
  118.8 8.7 %copy-start.30 = (f32[15,128]{1,0:T(8,128)}, f32[15,128]{1,0:T(8,128)S(1)}, u32[]{:S(2)}) copy-start(f32[15,128]{1,0:T(8,128)S(1)} %slice.1156) | copy-start | bytes 23044
  118.9 8.7 %copy-start.31 = (f32[15,128]{1,0:T(8,128)}, f32[15,128]{1,0:T(8,128)S(1)}, u32[]{:S(2)}) copy-start(f32[15,128]{1,0:T(8,128)S(1)} %slice.1083) | copy-start | bytes 23044
  118.9 9.2 %copy-start.45 = (f32[1,128]{1,0:T(1,128)S(1)}, f32[1,128]{1,0:T(1,128)}, u32[]{:S(2)}) copy-start(f32[1,128]{1,0:T(1,128)} %slice.1411) | copy-start | bytes 1540
  118.9 8.6 %copy-start.32 = (f32[15,128]{1,0:T(8,128)}, f32[15,128]{1,0:T(8,128)S(1)}, u32[]{:S(2)}) copy-start(f32[15,128]{1,0:T(8,128)S(1)} %slice.1148) | copy-start | bytes 23044
  118.9 8.5 %copy-start.33 = (f32[15,128]{1,0:T(8,128)}, f32[15,128]{1,0:T(8,128)S(1)}, u32[]{:S(2)}) copy-start(f32[15,128]{1,0:T(8,128)S(1)} %slice.1157) | copy-start | bytes 23044
  139.8 10.2 %copy-start.5 = (f32[127,128]{1,0:T(8,128)S(1)}, f32[127,128]{1,0:T(8,128)}, u32[]{:S(2)}) copy-start(f32[127,128]{1,0:T(8,128)} %copy-done.4) | copy-start | bytes 195076
  139.8 10.2 %copy-start.7 = (f32[127,128]{1,0:T(8,128)S(1)}, f32[127,128]{1,0:T(8,128)}, u32[]{:S(2)}) copy-start(f32[127,128]{1,0:T(8,128)} %copy-done.6) | copy-start | bytes 195076
  139.8 10.2 %copy-start.9 = (f32[127,128]{1,0:T(8,128)S(1)}, f32[127,128]{1,0:T(8,128)}, u32[]{:S(2)}) copy-start(f32[127,128]{1,0:T(8,128)} %copy-done.8) | copy-start | bytes 195076
  139.8 10.2 %copy-start.11 = (f32[127,128]{1,0:T(8,128)S(1)}, f32[127,128]{1,0:T(8,128)}, u32[]{:S(2)}) copy-start(f32[127,128]{1,0:T(8,128)} %copy-done.10) | copy-start | bytes 195076
  153.9 9.0 %copy-start.38 = (f32[1,128]{1,0:T(1,128)S(1)}, f32[1,128]{1,0:T(1,128)}, u32[]{:S(2)}) copy-start(f32[1,128]{1,0:T(1,128)} %slice.1375) | copy-start | bytes 1540
  153.9 12.9 %copy-start.39 = (f32[1,128]{1,0:T(1,128)S(1)}, f32[1,128]{1,0:T(1,128)}, u32[]{:S(2)}) copy-start(f32[1,128]{1,0:T(1,128)} %slice.1409) | copy-start | bytes 1540
  155.2 22.5 %copy-start.24 = (f32[256,128]{1,0:T(8,128)S(1)}, f32[256,128]{1,0:T(8,128)}, u32[]{:S(2)}) copy-start(f32[256,128]{1,0:T(8,128)} %add.1031) | copy-start | bytes 393220
  156.2 23.1 %copy-start.12 = (f32[512,128]{1,0:T(8,128)}, f32[512,128]{1,0:T(8,128)S(1)}, u32[]{:S(2)}) copy-start(f32[512,128]{1,0:T(8,128)S(1)} %pad.437) | copy-start | bytes 786436
  158.9 45.1 %copy-start.13 = (f32[512,128]{1,0:T(8,128)}, f32[512,128]{1,0:T(8,128)S(1)}, u32[]{:S(2)}) copy-start(f32[512,128]{1,0:T(8,128)S(1)} %pad.400) | copy-start | bytes 786436
  164.5 40.3 %copy-start.36 = (f32[2,128]{1,0:T(2,128)S(1)}, f32[2,128]{1,0:T(2,128)}, u32[]{:S(2)}) copy-start(f32[2,128]{1,0:T(2,128)} %param.10) | copy-start | bytes 3076
  182.8 21.0 %all-to-all-start = ((f32[32,6,128]{2,1,0:T(8,128)}), f32[32,6,128]{2,1,0:T(8,128)S(1)}, u32[]{:S(2)}, u32[]{:S(2)}) async-start(f32[32,6,128]{2,1,0:T(8,128)} %broadcast_in_dim.60), calls=%async_computation | async-start | bytes 262144 | tf_op jit(solution)/shard_map/all_to_all | solution.py:18
  244.5 55.8 %all-to-all-start.2 = ((bf16[8,512,256]{2,1,0:T(8,128)(2,1)}), bf16[8,512,256]{2,1,0:T(8,128)(2,1)}, u32[]{:S(2)}, u32[]{:S(2)}) async-start(bf16[8,512,256]{2,1,0:T(8,128)(2,1)} %copy.43), calls=%async_computation.2 | async-start | bytes 4194304 | tf_op jit(solution)/shard_map/all_to_all | solution.py:78
  (20 other events, 97.0 us)
Sparse Core Ops, SparseCore 0:
  10.0 55.5 all-gather.1
where the time goes:
time: 312 us; the launch traced here: 310 us
  waiting for transfers between devices  105 us (34%)
  local copies, waits for them, and re-layouts  101 us (32%)
  other arithmetic  49.8 us (16%)
  starting transfers between devices  19.2 us (6%)
  between operations  16.1 us (5%)
  blocking collectives  11.8 us (4%)
  matrix products  7.45 us (2%)
    all_to_all x1, waiting for transfers between devices, sum_in_two_steps(): lax.all_to_all(own.astype(jnp.bfloat16), far, 0, 0, tiled=True)  49.2 us
    slice x180, local copies, waits for them, and re-layouts, local(): cumulative = lax.associative_scan(compose, terms, axis=0)  46.3 us
    all_gather x1, waiting for transfers between devices, local(): lax.all_gather(inputs, MP, axis=1, tiled=True)  44.4 us
    pad x96, local copies, waits for them, and re-layouts, local(): cumulative = lax.associative_scan(compose, terms, axis=0)  22.9 us
    concatenate x48, other arithmetic, local(): cumulative = lax.associative_scan(compose, terms, axis=0)  16.2 us
    all_to_all x1, blocking collectives, sum_at_owner(): tiles = lax.all_to_all(cut_along(shard, dim, size), axis, 0, 0, tiled=True)  11.8 us
    all_to_all x1, waiting for transfers between devices, copy_for_each(): lax.all_to_all(jnp.broadcast_to(shard[None], (size, *shard.shape)), axis,...  10.7 us
    add x51, other arithmetic, local(): cumulative = lax.associative_scan(compose, terms, axis=0)  10.5 us
  transfers between devices with their start and end apart: 4, of which 3 were waited for; matrix products, arithmetic and copies ran while one was open for 4% of the time, Pallas kernels for 0%

commit v1 on v0

v1 whole, which is shorter than its diff:
```python
import jax
import jax.numpy as jnp
from jax import lax
from jax.experimental import pallas as pl
from jax.experimental.pallas import tpu as pltpu
from jax.sharding import PartitionSpec as P

MESH = pl.DeviceIdType.MESH
F32 = jnp.float32
BF16 = jnp.bfloat16

NY = 8
NX = 4
NZ = 8
NS = NX * NZ
ROWS = 512
BLK = 256
Q = 4
CH = ROWS // Q
SEG = CH // 8
STEPS = 14


def compose(later, earlier):
    a, b, c, d, e, f = later
    p, q, r, s, t, u = earlier
    return (
        a * p + b * r,
        a * q + b * s,
        c * p + d * r,
        c * q + d * s,
        a * t + b * u + e,
        c * t + d * u + f,
    )


def apply_map(m, state):
    a, b, c, d, e, f = m
    x, y = state
    return (a * x + b * y + e, c * x + d * y + f)


def kernel(
    x_hbm,
    g_hbm,
    init_hbm,
    w_hbm,
    bias_hbm,
    ang_hbm,
    str_hbm,
    wo_hbm,
    nsb,
    outb,
    xg,
    w2,
    wi,
    wtmp,
    wo,
    acc,
    gs,
    rot,
    terms,
    seg,
    tot,
    xbuf,
    rowtot,
    zbuf,
    stb,
    sbuf,
    rbuf,
    otmp,
    ini,
    bia,
    ang,
    stg,
    loc_sem,
    agi_recv,
    agd_recv,
    ag_send,
    d2d_send,
    g_sem,
    wo_sem,
    x_send,
    x_recv,
    z_send,
    z_recv,
    st_send,
    st_recv,
    rs_send,
    rs_recv,
):
    s = lax.axis_index("seq")
    m = lax.axis_index("mp")
    y = m // 2
    c = m % 2
    zi = s // NX
    xi = s % NX

    def ring(k):
        return lax.rem(y + k + 2 * NY, NY)

    def dev(seq, mp):
        return {"seq": seq, "mp": mp}

    up = dev(s, ring(1) * 2 + c)
    down = dev(s, ring(-1) * 2 + c)
    partner = dev(s, y * 2 + 1 - c)

    in_copy = pltpu.make_async_copy(x_hbm, xg.at[m], loc_sem.at[0])
    in_copy.start()
    w_copy = pltpu.make_async_copy(w_hbm, w2, loc_sem.at[1])
    w_copy.start()
    g_copy = pltpu.make_async_copy(g_hbm, gs.at[pl.ds(8, 2 * ROWS)], loc_sem.at[2])
    g_copy.start()
    small = [
        pltpu.make_async_copy(a, b, loc_sem.at[3 + i])
        for i, (a, b) in enumerate(
            ((init_hbm, ini), (bias_hbm, bia), (ang_hbm, ang), (str_hbm, stg))
        )
    ]
    for copy in small:
        copy.start()

    barrier = pltpu.get_barrier_semaphore()

    def greet(target):
        pl.semaphore_signal(barrier, inc=1, device_id=target, device_id_type=MESH)

    for target in (up, down, partner):
        greet(target)
    for dx in range(1, NX):
        greet(dev(zi * NX + lax.rem(xi + dx, NX), m))
    for dz in range(1, NZ):
        greet(dev(lax.rem(zi + dz, NZ) * NX + xi, m))
    greet(dev(lax.rem(s + 1, NS), m))
    greet(dev(lax.rem(s + NS - 1, NS), m))
    pl.semaphore_wait(barrier, 3 + (NX - 1) + (NZ - 1) + 2)

    def rows(q):
        return pl.ds(pl.multiple_of(q * CH, CH), CH)

    def ici(block, q, g, d, half):
        ref = xg.at[block, rows(q)]
        if half:
            ref = xg.at[block, rows(q), pl.ds(d * (BLK // 2), BLK // 2)]
        return pltpu.make_async_remote_copy(
            src_ref=ref,
            dst_ref=ref,
            send_sem=ag_send.at[0],
            recv_sem=agi_recv.at[d, g, q],
            device_id=(up, down)[d],
            device_id_type=MESH,
        )

    def d2d(block, q, g, d, half):
        ref = xg.at[block, rows(q)]
        if half:
            ref = xg.at[block, rows(q), pl.ds(d * (BLK // 2), BLK // 2)]
        return pltpu.make_async_remote_copy(
            src_ref=ref,
            dst_ref=ref,
            send_sem=d2d_send.at[0],
            recv_sem=agd_recv.at[d, g, q],
            device_id=partner,
            device_id_type=MESH,
        )

    in_copy.wait()
    for q in range(Q):
        for d in range(2):
            ici(m, q, 0, d, False).start()
    for q in range(Q):
        d2d(m, q, 0, 0, False).start()

    g_send = pltpu.make_async_remote_copy(
        src_ref=g_hbm.at[pl.ds(2 * ROWS - 8, 8)],
        dst_ref=gs.at[pl.ds(0, 8)],
        send_sem=g_sem.at[0],
        recv_sem=g_sem.at[1],
        device_id=dev(lax.rem(s + 1, NS), m),
        device_id_type=MESH,
    )

    @pl.when(s < NS - 1)
    def _():
        g_send.start()

    def wo_cols(k, core):
        return wo_hbm.at[:, pl.ds(pl.multiple_of((2 * k + core) * BLK, BLK), BLK)]

    for k in range(NY):
        pltpu.make_async_copy(wo_cols(k, c), wo.at[c, k], wo_sem.at[0]).start()
        pltpu.make_async_remote_copy(
            src_ref=wo_cols(k, 1 - c),
            dst_ref=wo.at[c, k],
            send_sem=wo_sem.at[1],
            recv_sem=wo_sem.at[2],
            device_id=partner,
            device_id_type=MESH,
        ).start()

    w_copy.wait()

    @pl.loop(0, 16)
    def _(b):
        wtmp[...] = w2[pl.ds(pl.multiple_of(b * 2 * BLK, 2 * BLK), 2 * BLK), :].astype(F32)
        for k in range(2):
            wi[b, :, k * 128 : (k + 1) * 128] = wtmp[pl.ds(k, BLK, stride=2), :].astype(BF16)

    for copy in small:
        copy.wait()
    cosine = jnp.broadcast_to(jnp.cos(ang[...]), (8, 128))
    sine = jnp.broadcast_to(jnp.sin(ang[...]), (8, 128))
    strength = jnp.broadcast_to(stg[...], (8, 128))

    bias_row = jnp.concatenate([bia[0:1, :], bia[1:2, :]], axis=1)
    other = y * 2 + 1 - c

    @pl.loop(0, Q)
    def _(q):
        d2d(other, q, 0, 0, False).wait_recv()
        r = rows(q)
        part = jnp.dot(xg[m, r, :], wi[m], preferred_element_type=F32)
        part += jnp.dot(xg[other, r, :], wi[other], preferred_element_type=F32)
        part += bias_row
        acc[0, r, :] = part[:, :128]
        acc[1, r, :] = part[:, 128:]

    def rotate_guess():
        g_copy.wait()

        @pl.when(s > 0)
        def _():
            g_send.wait_recv()

        @pl.when(s == 0)
        def _():
            gs[6:8, :] = ini[...]

        for q in range(Q):

            @pl.loop(0, SEG)
            def _(j):
                at = 6 + 2 * (q * CH + j)
                one = gs[pl.ds(at, 8, stride=2 * SEG), :]
                two = gs[pl.ds(at + 1, 8, stride=2 * SEG), :]
                rot[q, j, 0] = cosine * one - sine * two
                rot[q, j, 1] = sine * one + cosine * two

    def add_group(g, q):
        r = rows(q)
        part = None
        for d in range(2):
            pos = ring(-g if d == 0 else g)
            d2d(2 * pos + 1 - c, q, g, d, False).wait_recv()
            for core in range(2):
                b = 2 * pos + core
                term = jnp.dot(xg[b, r, :], wi[b], preferred_element_type=F32)
                part = term if part is None else part + term
        acc[0, r, :] += part[:, :128]
        acc[1, r, :] += part[:, 128:]

    for g in range(1, 4):

        @pl.loop(0, Q)
        def _(q):
            for d in range(2):
                b = 2 * ring(-g if d == 0 else g) + c
                ici(b, q, g - 1, d, False).wait_recv()
                ici(b, q, g, d, g == 3).start()
                d2d(b, q, g, d, False).start()
            if g > 1:
                add_group(g - 1, q)

        if g == 1:
            rotate_guess()

    @pl.loop(0, Q)
    def _(q):
        add_group(3, q)

    iota = lax.broadcasted_iota(jnp.int32, (8, 128), 0)
    one_v = jnp.ones((8, 128), F32)
    zero_v = jnp.zeros((8, 128), F32)
    identity = (one_v, zero_v, zero_v, one_v, zero_v, zero_v)

    def shifted(mm, k):
        return tuple(
            jnp.where(iota < k, ident, pltpu.roll(v, k, 0)) for v, ident in zip(mm, identity)
        )

    far = ring(4)

    @pl.loop(0, Q)
    def _(q):
        b = 2 * far + c
        for d in range(2):
            ici(b, q, 3, d, True).wait_recv()
            d2d(b, q, 4, d, True).start()
        r = rows(q)
        part = jnp.dot(xg[b, r, :], wi[b], preferred_element_type=F32)
        b2 = 2 * far + 1 - c
        for d in range(2):
            d2d(b2, q, 4, d, True).wait_recv()
        part += jnp.dot(xg[b2, r, :], wi[b2], preferred_element_type=F32)
        acc[0, r, :] += part[:, :128]
        acc[1, r, :] += part[:, 128:]
        mm = None
        for j in range(SEG):
            at = q * CH + j
            r1 = rot[q, j, 0]
            r2 = rot[q, j, 1]
            sq1 = jnp.tanh(r1 + acc[0, pl.ds(at, 8, stride=SEG), :])
            sq2 = jnp.tanh(r2 + acc[1, pl.ds(at, 8, stride=SEG), :])
            t1 = sq1 * sq1
            t2 = sq2 * sq2
            sl1 = 1.0 - strength * t1
            sl2 = 1.0 - strength * t2
            of1 = strength * (sq1 - r1 * (1.0 - t1))
            of2 = strength * (sq2 - r2 * (1.0 - t2))
            terms[q, j, 0] = sl1
            terms[q, j, 1] = sl2
            terms[q, j, 2] = of1
            terms[q, j, 3] = of2
            here = (sl1 * cosine, -sl1 * sine, sl2 * sine, sl2 * cosine, of1, of2)
            mm = here if mm is None else compose(here, mm)
        for k in (1, 2, 4):
            mm = compose(mm, shifted(mm, k))
        before = shifted(mm, 1)
        for i in range(6):
            seg[q, i] = before[i]
            seg[q, 6 + i] = jnp.broadcast_to(mm[i][7:8, :], (8, 128))

    def chunk_total(q):
        return tuple(seg[q, 6 + i] for i in range(6))

    whole = chunk_total(0)
    for q in range(1, Q):
        whole = compose(chunk_total(q), whole)
    for i in range(6):
        tot[i : i + 1, :] = whole[i][0:1, :]
    for i in range(6, 8):
        tot[i : i + 1, :] = jnp.zeros((1, 128), F32)

    def x_copy(dx):
        return pltpu.make_async_remote_copy(
            src_ref=tot,
            dst_ref=xbuf.at[dx],
            send_sem=x_send.at[dx],
            recv_sem=x_recv.at[dx],
            device_id=dev(zi * NX + lax.rem(xi + dx, NX), m),
            device_id_type=MESH,
        )

    for dx in range(1, NX):
        x_copy(dx).start()
    for dx in range(1, NX):
        x_copy(dx).wait_recv()

    def from_x(k):
        def member(i):
            value = whole[i]
            for dx in range(1, NX):
                here = lax.rem(xi - k + NX, NX) == dx
                value = jnp.where(here, jnp.broadcast_to(xbuf[dx, i : i + 1, :], (8, 128)), value)
            return value

        return tuple(member(i) for i in range(6))

    line = from_x(0)
    ahead = tuple(jnp.where(xi > 0, v, ident) for v, ident in zip(line, identity))
    for k in range(1, NX):
        mk = from_x(k)
        line = compose(mk, line)
        if k < NX - 1:
            more = compose(mk, ahead)
            ahead = tuple(jnp.where(xi > k, v, w) for v, w in zip(more, ahead))
    for i in range(6):
        rowtot[i : i + 1, :] = line[i][0:1, :]
    for i in range(6, 8):
        rowtot[i : i + 1, :] = jnp.zeros((1, 128), F32)

    def z_copy(dz):
        return pltpu.make_async_remote_copy(
            src_ref=rowtot,
            dst_ref=zbuf.at[dz],
            send_sem=z_send.at[dz],
            recv_sem=z_recv.at[dz],
            device_id=dev(lax.rem(zi + dz, NZ) * NX + xi, m),
            device_id_type=MESH,
        )

    for dz in range(1, NZ):

        @pl.when(zi + dz < NZ)
        def _():
            z_copy(dz).start()

    for dz in range(1, NZ):

        @pl.when(zi >= dz)
        def _():
            z_copy(dz).wait_recv()

    state = tuple(jnp.broadcast_to(ini[k : k + 1, :], (8, 128)) for k in range(2))
    for dz in range(NZ - 1, 0, -1):
        mk = tuple(jnp.broadcast_to(zbuf[dz, i : i + 1, :], (8, 128)) for i in range(6))
        after = apply_map(mk, state)
        state = tuple(jnp.where(zi >= dz, v, w) for v, w in zip(after, state))
    state = apply_map(ahead, state)

    entering = [state]
    for q in range(Q - 1):
        entering.append(apply_map(chunk_total(q), entering[-1]))
    current = [
        apply_map(tuple(seg[q, i] for i in range(6)), entering[q]) for q in range(Q)
    ]

    def st_copy(q, core):
        return pltpu.make_async_remote_copy(
            src_ref=stb.at[core, q],
            dst_ref=stb.at[core, q],
            send_sem=st_send.at[q],
            recv_sem=st_recv.at[q],
            device_id=partner,
            device_id_type=MESH,
        )

    for q in range(Q):
        pair = [[], []]
        x1, x2 = current[q]
        for j in range(SEG):
            u1 = cosine * x1 - sine * x2
            u2 = sine * x1 + cosine * x2
            x1 = terms[q, j, 0] * u1 + terms[q, j, 2]
            x2 = terms[q, j, 1] * u2 + terms[q, j, 3]
            at = 2 * (q * CH + j)
            nsb[pl.ds(at, 8, stride=2 * SEG), :] = x1
            nsb[pl.ds(at + 1, 8, stride=2 * SEG), :] = x2
            pair[0].append(x1)
            pair[1].append(x2)
            if j % 2 == 1:
                for k in range(2):
                    both = jnp.concatenate(pair[k], axis=0).astype(BF16)
                    stb[c, q, (j - 1) * 8 : (j + 1) * 8, k * 128 : (k + 1) * 128] = both
                pair = [[], []]
        st_copy(q, c).start()

    pltpu.make_async_copy(wo.at[c], wo.at[c], wo_sem.at[0]).wait()
    wo_all = pltpu.make_async_remote_copy(
        src_ref=wo.at[1 - c],
        dst_ref=wo.at[1 - c],
        send_sem=wo_sem.at[1],
        recv_sem=wo_sem.at[2],
        device_id=partner,
        device_id_type=MESH,
    )
    wo_all.wait_recv()
    for q in range(Q):
        st_copy(q, 1 - c).wait_recv()

    def own(k, q):
        part = jnp.dot(stb[0, q], wo[0, k], preferred_element_type=F32)
        return part + jnp.dot(stb[1, q], wo[1, k], preferred_element_type=F32)

    def rs_copy(d, i):
        return pltpu.make_async_remote_copy(
            src_ref=sbuf.at[d, i],
            dst_ref=rbuf.at[d, i],
            send_sem=rs_send.at[0],
            recv_sem=rs_recv.at[d, i],
            device_id=(up, down)[d],
            device_id_type=MESH,
        )

    @pl.loop(0, 4)
    def _(i):
        for d in range(2):
            dist = (17 - i) // 4
            k = ring(dist) if d == 0 else ring(-dist)
            q = lax.rem(i + 2 * d, Q)
            sbuf[d, i] = own(k, q).astype(BF16)
            rs_copy(d, i).start()

    @pl.loop(4, STEPS)
    def _(i):
        for d in range(2):
            dist = (17 - i) // 4
            k = ring(dist) if d == 0 else ring(-dist)
            q = lax.rem(i + 2 * d, Q)
            mine = own(k, q)
            rs_copy(d, i - 4).wait_recv()
            sbuf[d, i] = (mine + rbuf[d, i - 4].astype(F32)).astype(BF16)
            rs_copy(d, i).start()

    for q in (2, 0, 3, 1):
        mine = own(y, q)
        up_at = 10 + (q + 2) % 4
        down_at = 10 + q
        rs_copy(0, up_at).wait_recv()
        rs_copy(1, down_at).wait_recv()
        total = mine + rbuf[0, up_at].astype(F32) + rbuf[1, down_at].astype(F32)
        for j in range(SEG):
            for h in range(2):
                otmp[h, pl.ds(j, 8, stride=SEG), :] = total[
                    j * 8 : (j + 1) * 8, h * 128 : (h + 1) * 128
                ]
        for h in range(2):
            outb[q * CH : (q + 1) * CH, h * 128 : (h + 1) * 128] = otmp[h].astype(BF16)

    def sent(ref, sem):
        pltpu.make_async_remote_copy(
            src_ref=ref,
            dst_ref=ref,
            send_sem=sem,
            recv_sem=rs_recv.at[0, 0],
            device_id=partner,
            device_id_type=MESH,
        ).wait_send()

    sent(xg.at[pl.ds(0, 7)], ag_send.at[0])
    sent(xg.at[pl.ds(0, 8)], d2d_send.at[0])
    sent(sbuf, rs_send.at[0])
    wo_all.wait_send()

    @pl.when(s < NS - 1)
    def _():
        g_send.wait_send()

    for dx in range(1, NX):
        x_copy(dx).wait_send()
    for dz in range(1, NZ):

        @pl.when(zi + dz < NZ)
        def _():
            z_copy(dz).wait_send()

    for q in range(Q):
        st_copy(q, c).wait_send()


def local(inputs, guess, initial, w_in, bias, angle, strength, w_out):
    dma = pltpu.SemaphoreType.DMA
    hbm = pl.BlockSpec(memory_space=pltpu.HBM)
    vmem = pl.BlockSpec(memory_space=pltpu.VMEM)
    new_state, output = pl.pallas_call(
        kernel,
        out_shape=(
            jax.ShapeDtypeStruct((2 * ROWS, 128), F32),
            jax.ShapeDtypeStruct((ROWS, BLK), BF16),
        ),
        in_specs=[hbm] * 8,
        out_specs=(vmem, vmem),
        scratch_shapes=[
            pltpu.VMEM((16, ROWS, BLK), BF16),
            pltpu.VMEM((8192, 128), BF16),
            pltpu.VMEM((16, BLK, BLK), BF16),
            pltpu.VMEM((2 * BLK, 128), F32),
            pltpu.VMEM((2, NY, BLK, BLK), BF16),
            pltpu.VMEM((2, ROWS, 128), F32),
            pltpu.VMEM((8 + 2 * ROWS, 128), F32),
            pltpu.VMEM((Q, SEG, 2, 8, 128), F32),
            pltpu.VMEM((Q, SEG, 4, 8, 128), F32),
            pltpu.VMEM((Q, 12, 8, 128), F32),
            pltpu.VMEM((8, 128), F32),
            pltpu.VMEM((NX, 8, 128), F32),
            pltpu.VMEM((8, 128), F32),
            pltpu.VMEM((NZ, 8, 128), F32),
            pltpu.VMEM((2, Q, CH, BLK), BF16),
            pltpu.VMEM((2, STEPS, CH, BLK), BF16),
            pltpu.VMEM((2, STEPS, CH, BLK), BF16),
            pltpu.VMEM((2, CH, 128), F32),
            pltpu.VMEM((2, 128), F32),
            pltpu.VMEM((2, 128), F32),
            pltpu.VMEM((1, 128), F32),
            pltpu.VMEM((1, 128), F32),
            dma((7,)),
            dma((2, 4, Q)),
            dma((2, 5, Q)),
            dma((1,)),
            dma((1,)),
            dma((2,)),
            dma((3,)),
            dma((NX,)),
            dma((NX,)),
            dma((NZ,)),
            dma((NZ,)),
            dma((Q,)),
            dma((Q,)),
            dma((1,)),
            dma((2, STEPS)),
        ],
        compiler_params=pltpu.CompilerParams(
            collective_id=0, has_side_effects=True, vmem_limit_bytes=48 * 1024 * 1024
        ),
    )(*(pltpu.with_memory_space_constraint(v, pltpu.HBM) for v in (
        inputs,
        guess.reshape(2 * ROWS, 128),
        initial,
        w_in.reshape(8192, 128),
        bias,
        angle.reshape(1, 128),
        strength.reshape(1, 128),
        w_out.reshape(BLK, 4096),
    )))
    return new_state.reshape(ROWS, 2, 128), output


def solution(mesh):
    placed = (
        P("seq", "mp"),
        P("seq", None, "mp"),
        P(None, "mp"),
        P(None, None, "mp"),
        P(None, "mp"),
        P("mp"),
        P("mp"),
        P(None, "mp", None),
    )
    return jax.shard_map(
        local,
        mesh=mesh,
        in_specs=placed,
        out_specs=(P("seq", None, "mp"), P("seq", "mp")),
        check_vma=False,
    )
```

time: 312 us -> 72 us (0.23)
  the two profiles are of different devices: /device:TPU:8 before, /device:TPU:81 now
where the time goes in v1:
time: 72 us; the launch traced here: 71.9 us
  Pallas kernels  69.8 us (97%)
  local copies, waits for them, and re-layouts  1.5 us (2%)
    pallas_call x1, Pallas kernels, local(): pl.pallas_call(kernel, out_shape=(jax.ShapeDtypeStruct((2 * ROWS, 128), F...  69.8 us
    unnamed x2, local copies, waits for them, and re-layouts  1.5 us

profile of v1, /device:TPU:81, one launch (start us, length us, event | category | flops | bytes accessed | tf_op | source)
XLA Modules:
  0.0 71.9 jit_solution(10553434688176710090)
XLA Ops:
  0.6 69.8 %shard_map.95 = (f32[1024,128]{1,0:T(8,128)S(1)}, bf16[512,256]{1,0:T(8,128)(2,1)S(1)}) custom-call(bf16[512,256]{1,0:T(8,128)(2,1)} %x_hbm.1, f32[1024,128]{1,0:T(8,128)} %bitcast.9, f32[2,128]{1,0:T(2,128)} %init_hbm.1, bf16[8192,128]{1,0:T(8,128)(2,1)} %bitcast.7, f32[2,128]{1,0:T(2,128)} %bias_hbm.1, f32[1,128]{1,0:T(1,128)} %bitcast.10, ...), custom_call_target="tpu_custom_call" | custom-call | tf_op jit(solution)/shard_map/pallas_call | solution.py:546
  70.4 0.8 %copy.12 = f32[512,2,128]{2,1,0:T(2,128)} copy(f32[512,2,128]{2,1,0:T(2,128)S(1)} %bitcast.6) | data formatting | bytes 1048576
  71.2 0.7 copy.13

commit v2 on v1

--- a/solution.py
+++ b/solution.py
@@ -88,6 +88,7 @@
     st_recv,
     rs_send,
     rs_recv,
+    ready,
 ):
     s = lax.axis_index("seq")
     m = lax.axis_index("mp")
@@ -129,12 +130,41 @@
     for target in (up, down, partner):
         greet(target)
     for dx in range(1, NX):
-        greet(dev(zi * NX + lax.rem(xi + dx, NX), m))
+
+        @pl.when(xi + dx < NX)
+        def _():
+            greet(dev(s + dx, m))
+
     for dz in range(1, NZ):
-        greet(dev(lax.rem(zi + dz, NZ) * NX + xi, m))
-    greet(dev(lax.rem(s + 1, NS), m))
-    greet(dev(lax.rem(s + NS - 1, NS), m))
-    pl.semaphore_wait(barrier, 3 + (NX - 1) + (NZ - 1) + 2)
+
+        @pl.when(zi + dz < NZ)
+        def _():
+            greet(dev(s + dz * NX, m))
+
+    @pl.when(s < NS - 1)
+    def _():
+        greet(dev(s + 1, m))
+
+    pl.semaphore_wait(barrier, 3 + xi + zi + lax.min(s, 1))
+
+    def answer(sem, target):
+        pl.semaphore_signal(sem, inc=1, device_id=target, device_id_type=MESH)
+
+    @pl.when(s > 0)
+    def _():
+        answer(ready.at[0], dev(s - 1, m))
+
+    for dx in range(1, NX):
+
+        @pl.when(xi >= dx)
+        def _():
+            answer(ready.at[1], dev(s - dx, m))
+
+    for dz in range(1, NZ):
+
+        @pl.when(zi >= dz)
+        def _():
+            answer(ready.at[2], dev(s - dz * NX, m))
 
     def rows(q):
         return pl.ds(pl.multiple_of(q * CH, CH), CH)
@@ -181,10 +211,6 @@
         device_id_type=MESH,
     )
 
-    @pl.when(s < NS - 1)
-    def _():
-        g_send.start()
-
     def wo_cols(k, core):
         return wo_hbm.at[:, pl.ds(pl.multiple_of((2 * k + core) * BLK, BLK), BLK)]
 
@@ -199,25 +225,27 @@
             device_id_type=MESH,
         ).start()
 
-    w_copy.wait()
-
-    @pl.loop(0, 16)
-    def _(b):
+    def prepare(b):
         wtmp[...] = w2[pl.ds(pl.multiple_of(b * 2 * BLK, 2 * BLK), 2 * BLK), :].astype(F32)
         for k in range(2):
             wi[b, :, k * 128 : (k + 1) * 128] = wtmp[pl.ds(k, BLK, stride=2), :].astype(BF16)
+
+    other = y * 2 + 1 - c
+    far = ring(4)
+    w_copy.wait()
+
+    @pl.loop(0, 4)
+    def _(i):
+        prepare(2 * ring((i // 2) * 4) + lax.rem(i, 2))
 
     for copy in small:
         copy.wait()
     cosine = jnp.broadcast_to(jnp.cos(ang[...]), (8, 128))
     sine = jnp.broadcast_to(jnp.sin(ang[...]), (8, 128))
     strength = jnp.broadcast_to(stg[...], (8, 128))
-
     bias_row = jnp.concatenate([bia[0:1, :], bia[1:2, :]], axis=1)
-    other = y * 2 + 1 - c
-
-    @pl.loop(0, Q)
-    def _(q):
+
+    def start_group(q):
         d2d(other, q, 0, 0, False).wait_recv()
         r = rows(q)
         part = jnp.dot(xg[m, r, :], wi[m], preferred_element_type=F32)
@@ -226,26 +254,14 @@
         acc[0, r, :] = part[:, :128]
         acc[1, r, :] = part[:, 128:]
 
-    def rotate_guess():
-        g_copy.wait()
-
-        @pl.when(s > 0)
-        def _():
-            g_send.wait_recv()
-
-        @pl.when(s == 0)
-        def _():
-            gs[6:8, :] = ini[...]
-
-        for q in range(Q):
-
-            @pl.loop(0, SEG)
-            def _(j):
-                at = 6 + 2 * (q * CH + j)
-                one = gs[pl.ds(at, 8, stride=2 * SEG), :]
-                two = gs[pl.ds(at + 1, 8, stride=2 * SEG), :]
-                rot[q, j, 0] = cosine * one - sine * two
-                rot[q, j, 1] = sine * one + cosine * two
+    def rotate_guess(q):
+        @pl.loop(0, SEG)
+        def _(j):
+            at = 6 + 2 * (q * CH + j)
+            one = gs[pl.ds(at, 8, stride=2 * SEG), :]
+            two = gs[pl.ds(at + 1, 8, stride=2 * SEG), :]
+            rot[q, j, 0] = cosine * one - sine * two
+            rot[q, j, 1] = sine * one + cosine * two
 
     def add_group(g, q):
         r = rows(q)
@@ -260,7 +276,27 @@
         acc[0, r, :] += part[:, :128]
         acc[1, r, :] += part[:, 128:]
 
+    def prepare_group(g, q):
+        prepare(2 * ring(jnp.where(q < 2, -g, g)) + lax.rem(q, 2))
+
     for g in range(1, 4):
+        if g == 2:
+
+            @pl.when(s < NS - 1)
+            def _():
+                pl.semaphore_wait(ready.at[0], 1)
+                g_send.start()
+
+        if g == 3:
+            g_copy.wait()
+
+            @pl.when(s > 0)
+            def _():
+                g_send.wait_recv()
+
+            @pl.when(s == 0)
+            def _():
+                gs[6:8, :] = ini[...]
 
         @pl.loop(0, Q)
         def _(q):
@@ -269,15 +305,21 @@
                 ici(b, q, g - 1, d, False).wait_recv()
                 ici(b, q, g, d, g == 3).start()
                 d2d(b, q, g, d, False).start()
-            if g > 1:
-                add_group(g - 1, q)
-
-        if g == 1:
-            rotate_guess()
-
-    @pl.loop(0, Q)
-    def _(q):
-        add_group(3, q)
+            if g == 1:
+                start_group(q)
+                prepare_group(1, q)
+                prepare_group(2, q)
+            if g == 2:
+                add_group(1, q)
+                prepare_group(3, q)
+            if g == 3:
+                add_group(2, q)
+
+                @pl.when(q > 0)
+                def _():
+                    add_group(3, q - 1)
+
+                rotate_guess(q)
 
     iota = lax.broadcasted_iota(jnp.int32, (8, 128), 0)
     one_v = jnp.ones((8, 128), F32)
@@ -289,14 +331,14 @@
             jnp.where(iota < k, ident, pltpu.roll(v, k, 0)) for v, ident in zip(mm, identity)
         )
 
-    far = ring(4)
-
-    @pl.loop(0, Q)
-    def _(q):
+    def far_arrives(q):
         b = 2 * far + c
         for d in range(2):
             ici(b, q, 3, d, True).wait_recv()
             d2d(b, q, 4, d, True).start()
+
+    def scan_chunk(q):
+        b = 2 * far + c
         r = rows(q)
         part = jnp.dot(xg[b, r, :], wi[b], preferred_element_type=F32)
         b2 = 2 * far + 1 - c
@@ -331,6 +373,20 @@
             seg[q, i] = before[i]
             seg[q, 6 + i] = jnp.broadcast_to(mm[i][7:8, :], (8, 128))
 
+    @pl.loop(0, Q + 1)
+    def _(q):
+        @pl.when(q < Q)
+        def _():
+            far_arrives(q)
+
+        @pl.when(q == 0)
+        def _():
+            add_group(3, Q - 1)
+
+        @pl.when(q > 0)
+        def _():
+            scan_chunk(q - 1)
+
     def chunk_total(q):
         return tuple(seg[q, 6 + i] for i in range(6))
 
@@ -351,6 +407,10 @@
             device_id=dev(zi * NX + lax.rem(xi + dx, NX), m),
             device_id_type=MESH,
         )
+
+    @pl.when(xi < NX - 1)
+    def _():
+        pl.semaphore_wait(ready.at[1], NX - 1 - xi)
 
     for dx in range(1, NX):
         x_copy(dx).start()
@@ -390,6 +450,10 @@
             device_id_type=MESH,
         )
 
+    @pl.when(zi < NZ - 1)
+    def _():
+        pl.semaphore_wait(ready.at[2], NZ - 1 - zi)
+
     for dz in range(1, NZ):
 
         @pl.when(zi + dz < NZ)
@@ -426,25 +490,29 @@
             device_id_type=MESH,
         )
 
-    for q in range(Q):
-        pair = [[], []]
-        x1, x2 = current[q]
+    for duo in ((0, 2), (1, 3)):
+        states = {q: current[q] for q in duo}
+        pairs = {q: ([], []) for q in duo}
         for j in range(SEG):
-            u1 = cosine * x1 - sine * x2
-            u2 = sine * x1 + cosine * x2
-            x1 = terms[q, j, 0] * u1 + terms[q, j, 2]
-            x2 = terms[q, j, 1] * u2 + terms[q, j, 3]
-            at = 2 * (q * CH + j)
-            nsb[pl.ds(at, 8, stride=2 * SEG), :] = x1
-            nsb[pl.ds(at + 1, 8, stride=2 * SEG), :] = x2
-            pair[0].append(x1)
-            pair[1].append(x2)
-            if j % 2 == 1:
-                for k in range(2):
-                    both = jnp.concatenate(pair[k], axis=0).astype(BF16)
-                    stb[c, q, (j - 1) * 8 : (j + 1) * 8, k * 128 : (k + 1) * 128] = both
-                pair = [[], []]
-        st_copy(q, c).start()
+            for q in duo:
+                x1, x2 = states[q]
+                u1 = cosine * x1 - sine * x2
+                u2 = sine * x1 + cosine * x2
+                x1 = terms[q, j, 0] * u1 + terms[q, j, 2]
+                x2 = terms[q, j, 1] * u2 + terms[q, j, 3]
+                states[q] = (x1, x2)
+                at = 2 * (q * CH + j)
+                nsb[pl.ds(at, 8, stride=2 * SEG), :] = x1
+                nsb[pl.ds(at + 1, 8, stride=2 * SEG), :] = x2
+                pairs[q][0].append(x1)
+                pairs[q][1].append(x2)
+                if j % 2 == 1:
+                    for k in range(2):
+                        both = jnp.concatenate(pairs[q][k], axis=0).astype(BF16)
+                        stb[c, q, (j - 1) * 8 : (j + 1) * 8, k * 128 : (k + 1) * 128] = both
+                    pairs[q] = ([], [])
+        for q in duo:
+            st_copy(q, c).start()
 
     pltpu.make_async_copy(wo.at[c], wo.at[c], wo_sem.at[0]).wait()
     wo_all = pltpu.make_async_remote_copy(
@@ -456,8 +524,6 @@
         device_id_type=MESH,
     )
     wo_all.wait_recv()
-    for q in range(Q):
-        st_copy(q, 1 - c).wait_recv()
 
     def own(k, q):
         part = jnp.dot(stb[0, q], wo[0, k], preferred_element_type=F32)
@@ -479,6 +545,11 @@
             dist = (17 - i) // 4
             k = ring(dist) if d == 0 else ring(-dist)
             q = lax.rem(i + 2 * d, Q)
+
+            @pl.when(i < 2)
+            def _():
+                st_copy(q, 1 - c).wait_recv()
+
             sbuf[d, i] = own(k, q).astype(BF16)
             rs_copy(d, i).start()
 
@@ -589,6 +660,7 @@
             dma((Q,)),
             dma((1,)),
             dma((2, STEPS)),
+            pltpu.SemaphoreType.REGULAR((3,)),
         ],
         compiler_params=pltpu.CompilerParams(
             collective_id=0, has_side_effects=True, vmem_limit_bytes=48 * 1024 * 1024

time: 72 us -> 62.5 us (0.87)
  the two profiles are of different devices: /device:TPU:81 before, /device:TPU:449 now
where the time goes in v2:
time: 62.5 us; the launch traced here: 62.4 us
  Pallas kernels  60.2 us (96%)
  local copies, waits for them, and re-layouts  1.5 us (2%)
  between operations  0.64 us (1%)
    pallas_call x1, Pallas kernels, local(): pl.pallas_call(kernel, out_shape=(jax.ShapeDtypeStruct((2 * ROWS, 128), F...  60.2 us
    unnamed x2, local copies, waits for them, and re-layouts  1.5 us

profile of v2, /device:TPU:449, one launch (start us, length us, event | category | flops | bytes accessed | tf_op | source)
XLA Modules:
  0.0 62.4 jit_solution(5886357003651172055)
XLA Ops:
  0.6 60.2 %shard_map.95 = (f32[1024,128]{1,0:T(8,128)S(1)}, bf16[512,256]{1,0:T(8,128)(2,1)S(1)}) custom-call(bf16[512,256]{1,0:T(8,128)(2,1)} %x_hbm.1, f32[1024,128]{1,0:T(8,128)} %bitcast.9, f32[2,128]{1,0:T(2,128)} %init_hbm.1, bf16[8192,128]{1,0:T(8,128)(2,1)} %bitcast.7, f32[2,128]{1,0:T(2,128)} %bias_hbm.1, f32[1,128]{1,0:T(1,128)} %bitcast.10, ...), custom_call_target="tpu_custom_call" | custom-call | tf_op jit(solution)/shard_map/pallas_call | solution.py:617
  60.9 0.8 %copy.12 = f32[512,2,128]{2,1,0:T(2,128)} copy(f32[512,2,128]{2,1,0:T(2,128)S(1)} %bitcast.6) | data formatting | bytes 1048576
  61.7 0.7 %copy.13 = bf16[512,256]{1,0:T(8,128)(2,1)} copy(bf16[512,256]{1,0:T(8,128)(2,1)S(1)} %get-tuple-element.9) | data formatting | bytes 524288

commit v3 on v0

v3 whole, which is shorter than its diff:
```python
import jax
import jax.numpy as jnp
from jax import lax
from jax.experimental import pallas as pl
from jax.experimental.pallas import tpu as pltpu
from jax.sharding import PartitionSpec as P

MESH = pl.DeviceIdType.MESH
F32 = jnp.float32
BF16 = jnp.bfloat16

NY = 8
NX = 4
NZ = 8
NS = NX * NZ
ROWS = 512
BLK = 256
HALF = ROWS // 2
TALL = HALF // 2
Q = 4
CH = HALF // Q
SEG = CH // 8
STEPS = 14


def compose(later, earlier):
    a, b, c, d, e, f = later
    p, q, r, s, t, u = earlier
    return (
        a * p + b * r,
        a * q + b * s,
        c * p + d * r,
        c * q + d * s,
        a * t + b * u + e,
        c * t + d * u + f,
    )


def apply_map(m, state):
    a, b, c, d, e, f = m
    x, y = state
    return (a * x + b * y + e, c * x + d * y + f)


def kernel(
    x_hbm,
    g_hbm,
    init_hbm,
    w_hbm,
    bias_hbm,
    ang_hbm,
    str_hbm,
    wo_hbm,
    nsb,
    outb,
    xg,
    w2,
    wi,
    wtmp,
    wo,
    acc,
    gs,
    rot,
    terms,
    seg,
    xbuf,
    rowtot,
    zbuf,
    nst,
    stb,
    sbuf,
    rbuf,
    fbuf,
    pbuf,
    obuf,
    fin,
    otmp,
    ini,
    bia,
    ang,
    stg,
    loc_sem,
    small_send,
    small_recv,
    first_sem,
    ag_recv,
    far_recv,
    ag_send,
    wi_send,
    wi_recv,
    g_sem,
    e_send,
    e_recv,
    wo_sem,
    x_send,
    x_recv,
    z_send,
    z_recv,
    ns_sem,
    o_send,
    o_recv,
    rs_send,
    rs_recv,
    f_recv,
    ready,
):
    s = lax.axis_index("seq")
    m = lax.axis_index("mp")
    y = m // 2
    c = m % 2
    zi = s // NX
    xi = s % NX

    def ring(k):
        return lax.rem(y + k + 2 * NY, NY)

    def dev(seq, mp):
        return {"seq": seq, "mp": mp}

    def remote(src, dst, send, recv, target):
        return pltpu.make_async_remote_copy(
            src_ref=src,
            dst_ref=dst,
            send_sem=send,
            recv_sem=recv,
            device_id=target,
            device_id_type=MESH,
        )

    o = 1 - c
    other = 2 * y + o
    up = dev(s, ring(1) * 2 + c)
    down = dev(s, ring(-1) * 2 + c)
    partner = dev(s, other)

    barrier = pltpu.get_barrier_semaphore()

    def greet(target):
        pl.semaphore_signal(barrier, inc=1, device_id=target, device_id_type=MESH)

    greet(partner)
    for core in range(2):
        greet(dev(s, ring(1) * 2 + core))
        greet(dev(s, ring(-1) * 2 + core))

    def half_rows(core):
        return pl.ds(pl.multiple_of(core * HALF, HALF), HALF)

    in_copy = pltpu.make_async_copy(x_hbm.at[half_rows(c)], xg.at[m], loc_sem.at[0])
    in_copy.start()
    w_copy = pltpu.make_async_copy(w_hbm, w2, loc_sem.at[1])
    w_copy.start()
    small = ((init_hbm, ini), (bias_hbm, bia), (ang_hbm, ang), (str_hbm, stg))
    small_copies = [
        pltpu.make_async_copy(a, b.at[c], loc_sem.at[2 + i]) for i, (a, b) in enumerate(small)
    ]
    for copy in small_copies:
        copy.start()

    for dx in range(1, NX):

        @pl.when(xi + dx < NX)
        def _():
            for core in range(2):
                greet(dev(s + dx, 2 * y + core))

    for dz in range(1, NZ):

        @pl.when(zi + dz < NZ)
        def _():
            greet(dev(s + dz * NX, m))

    @pl.when(s < NS - 1)
    def _():
        greet(dev(s + 1, 2 * y))

    pl.semaphore_wait(barrier, 5 + 2 * xi + zi + 2 * (lax.min(s, 1) * o))

    def answer(sem, target):
        pl.semaphore_signal(sem, inc=1, device_id=target, device_id_type=MESH)

    def block_of(pos, a):
        return 2 * pos + jnp.where(a < 2, c, o)

    def tall(h):
        return pl.ds(pl.multiple_of(h * TALL, TALL), TALL)

    def ici(pos, a, g, d):
        ref = xg.at[block_of(pos, a), tall(lax.rem(a, 2))]
        return remote(ref, ref, ag_send.at[0], ag_recv.at[d, g, a], (up, down)[d])

    def far_piece(pos, slot, d):
        columns = pl.ds(d * 128, 128)
        if slot < 2:
            ref = xg.at[2 * pos + c, pl.ds(slot * TALL, TALL), columns]
        else:
            ref = xg.at[2 * pos + o, pl.ds((slot - 2) * CH, CH), columns]
        return remote(ref, ref, ag_send.at[0], far_recv.at[d, slot], (up, down)[d])

    first = remote(
        x_hbm.at[half_rows(o)], xg.at[m], first_sem.at[0], first_sem.at[1], partner
    )
    first.start()
    in_copy.wait()
    for a in range(2):
        for d in range(2):
            ici(y, a, 0, d).start()

    def small_copy(i):
        a, b = small[i]
        return remote(a, b.at[c], small_send.at[i], small_recv.at[i], partner)

    for i in range(4):
        small_copy(i).start()

    @pl.when((s > 0) & (c == 0))
    def _():
        answer(ready.at[0], dev(s - 1, 2 * y))
        answer(ready.at[0], dev(s - 1, 2 * y + 1))

    for dx in range(1, NX):

        @pl.when(xi >= dx)
        def _():
            for core in range(2):
                answer(ready.at[1], dev(s - dx, 2 * y + core))

    for dz in range(1, NZ):

        @pl.when(zi >= dz)
        def _():
            answer(ready.at[2], dev(s - dz * NX, m))

    def guess_own(core):
        if core == 0:
            return pltpu.make_async_copy(
                g_hbm.at[pl.ds(0, 2 * HALF)], gs.at[0, pl.ds(8, 2 * HALF)], loc_sem.at[6]
            )
        return pltpu.make_async_copy(
            g_hbm.at[pl.ds(2 * HALF - 8, 2 * HALF + 8)], gs.at[1], loc_sem.at[6]
        )

    def guess_to(core):
        pb = 1 - core
        if core == 0:
            return remote(
                g_hbm.at[pl.ds(0, 2 * HALF)],
                gs.at[pb, pl.ds(8, 2 * HALF)],
                g_sem.at[0],
                g_sem.at[1],
                partner,
            )
        return remote(
            g_hbm.at[pl.ds(2 * HALF - 8, 2 * HALF + 8)],
            gs.at[pb],
            g_sem.at[0],
            g_sem.at[1],
            partner,
        )

    first_recv = first.wait_recv
    w_copy.wait()

    def prepare(b):
        wtmp[...] = w2[pl.ds(pl.multiple_of(b * 2 * BLK, 2 * BLK), 2 * BLK), :].astype(F32)
        for k in range(2):
            wi[c, b, :, k * 128 : (k + 1) * 128] = wtmp[pl.ds(k, BLK, stride=2), :].astype(BF16)
        wi_copy(c, b).start()

    def wi_copy(pb, b):
        return remote(wi.at[pb, b], wi.at[pb, b], wi_send.at[0], wi_recv.at[b], partner)

    prepare(m)
    first_recv()
    for a in range(2, 4):
        for d in range(2):
            ici(y, a, 0, d).start()
    prepare(other)

    for core in range(2):

        @pl.when(c == core)
        def _():
            guess_own(core).start()
            guess_to(1 - core).start()

    far = ring(4)
    prepare(2 * far)
    prepare(2 * far + 1)

    for copy in small_copies:
        copy.wait()
    for i in range(4):
        small_copy(i).wait_recv()

    def lanes(v):
        return jnp.broadcast_to(v, (8, 128))

    cosine = [lanes(jnp.cos(ang[pb])) for pb in range(2)]
    sine = [lanes(jnp.sin(ang[pb])) for pb in range(2)]
    strength = [lanes(stg[pb]) for pb in range(2)]

    def products(b, r):
        lhs = xg[b, r, :]
        return [jnp.dot(lhs, wi[pb, b], preferred_element_type=F32) for pb in range(2)]

    def start_group(h):
        r = tall(h)

        @pl.when(h == 0)
        def _():
            wi_copy(o, m).wait_recv()
            wi_copy(o, other).wait_recv()

        one = products(m, r)
        two = products(other, r)
        for pb in range(2):
            part = one[pb] + two[pb]
            acc[2 * pb, r, :] = part[:, :128] + bia[pb, 0:1, :]
            acc[2 * pb + 1, r, :] = part[:, 128:] + bia[pb, 1:2, :]

    def add_blocks(blocks, r):
        part = None
        for b in blocks:
            term = products(b, r)
            part = term if part is None else [u + v for u, v in zip(part, term)]
        for pb in range(2):
            acc[2 * pb, r, :] += part[pb][:, :128]
            acc[2 * pb + 1, r, :] += part[pb][:, 128:]

    def add_group(g, h):
        blocks = [2 * ring(k) + core for k in (-g, g) for core in range(2)]

        def weights():
            for b in blocks:
                wi_copy(o, b).wait_recv()

        if isinstance(h, int):
            if h == 0:
                weights()
            add_blocks(blocks, pl.ds(h * TALL, TALL))
        else:
            pl.when(h == 0)(weights)
            add_blocks(blocks, tall(h))

    def rotate_guess(q):
        @pl.loop(0, SEG)
        def _(j):
            at = 6 + 2 * (q * CH + j)
            for pb in range(2):
                one = gs[pb, pl.ds(at, 8, stride=2 * SEG), :]
                two = gs[pb, pl.ds(at + 1, 8, stride=2 * SEG), :]
                rot[q, j, 2 * pb] = cosine[pb] * one - sine[pb] * two
                rot[q, j, 2 * pb + 1] = sine[pb] * one + cosine[pb] * two

    def prepare_group(g, i):
        prepare(2 * ring(jnp.where(i < 2, -g, g)) + lax.rem(i, 2))

    def edge(pb):
        return remote(
            g_hbm.at[pl.ds(2 * ROWS - 8, 8)],
            gs.at[pb, pl.ds(0, 8)],
            e_send.at[0],
            e_recv.at[pb],
            dev(lax.rem(s + 1, NS), 2 * y),
        )

    def wo_cols(k):
        return wo_hbm.at[:, pl.ds(k * BLK, BLK)]

    def wo_copy(k):
        return remote(wo_cols(k), wo.at[c, k], wo_sem.at[1], wo_sem.at[2], partner)

    for g in range(1, 4):
        if g == 2:
            for k in range(2 * NY):
                pltpu.make_async_copy(wo_cols(k), wo.at[c, k], wo_sem.at[0]).start()
                wo_copy(k).start()

            @pl.when(s < NS - 1)
            def _():
                pl.semaphore_wait(ready.at[0], 1)
                edge(c).start()

        if g == 3:
            for core in range(2):

                @pl.when(c == core)
                def _():
                    guess_own(core).wait()
                    guess_to(core).wait_recv()

            @pl.when((s > 0) & (c == 0))
            def _():
                for pb in range(2):
                    edge(pb).wait_recv()

            @pl.when((s == 0) & (c == 0))
            def _():
                for pb in range(2):
                    gs[pb, 6:8, :] = ini[pb]

            for a in range(4):
                for d in range(2):
                    pos = ring(-3 if d == 0 else 3)
                    ici(pos, a, 2, d).wait_recv()
                    for slot in ((0,), (1,), (2, 3), (4, 5))[a]:
                        far_piece(pos, slot, d).start()
                if a < 2:
                    add_group(2, a)
                if a == 3:
                    add_group(3, 0)
                rotate_guess(a)
        else:

            @pl.loop(0, 4)
            def _(a):
                for d in range(2):
                    pos = ring(-g if d == 0 else g)
                    ici(pos, a, g - 1, d).wait_recv()
                    ici(pos, a, g, d).start()
                if g == 1:
                    prepare_group(1, a)
                    prepare_group(2, a)
                else:
                    prepare_group(3, a)

                @pl.when(lax.rem(a, 2) == 1)
                def _():
                    if g == 1:
                        start_group(a // 2)
                    else:
                        add_group(1, a // 2)

    iota = lax.broadcasted_iota(jnp.int32, (8, 128), 0)
    one_v = jnp.ones((8, 128), F32)
    zero_v = jnp.zeros((8, 128), F32)
    identity = (one_v, zero_v, zero_v, one_v, zero_v, zero_v)

    def shifted(mm, k):
        return tuple(
            jnp.where(iota < k, ident, pltpu.roll(v, k, 0)) for v, ident in zip(mm, identity)
        )

    def scan_chunk(q):
        for d in range(2):
            for slot in ((0, 2), (3,), (1, 4), (5,))[q]:
                far_piece(far, slot, d).wait_recv()
        if q == 0:
            add_group(3, 1)
            wi_copy(o, 2 * far).wait_recv()
            wi_copy(o, 2 * far + 1).wait_recv()
        add_blocks((2 * far, 2 * far + 1), pl.ds(q * CH, CH))
        mm = [None, None]
        for j in range(SEG):
            at = q * CH + j
            for pb in range(2):
                st = strength[pb]
                r1 = rot[q, j, 2 * pb]
                r2 = rot[q, j, 2 * pb + 1]
                sq1 = jnp.tanh(r1 + acc[2 * pb, pl.ds(at, 8, stride=SEG), :])
                sq2 = jnp.tanh(r2 + acc[2 * pb + 1, pl.ds(at, 8, stride=SEG), :])
                t1 = sq1 * sq1
                t2 = sq2 * sq2
                sl1 = 1.0 - st * t1
                sl2 = 1.0 - st * t2
                of1 = st * (sq1 - r1 * (1.0 - t1))
                of2 = st * (sq2 - r2 * (1.0 - t2))
                for i, v in enumerate((sl1, sl2, of1, of2)):
                    terms[q, j, 4 * pb + i] = v
                co, si = cosine[pb], sine[pb]
                here = (sl1 * co, -sl1 * si, sl2 * si, sl2 * co, of1, of2)
                mm[pb] = here if mm[pb] is None else compose(here, mm[pb])
        for k in (1, 2, 4):
            mm = [compose(v, shifted(v, k)) for v in mm]
        for pb in range(2):
            before = shifted(mm[pb], 1)
            for i in range(6):
                seg[q, pb, i] = before[i]
                seg[q, pb, 6 + i] = lanes(mm[pb][i][7:8, :])

    for q in range(Q):
        scan_chunk(q)

    def chunk_total(q, pb):
        return tuple(seg[q, pb, 6 + i] for i in range(6))

    place = 2 * xi + c
    for pb in range(2):
        whole = chunk_total(0, pb)
        for q in range(1, Q):
            whole = compose(chunk_total(q, pb), whole)
        for i in range(6):
            xbuf[place, 6 * pb + i : 6 * pb + i + 1, :] = whole[i][0:1, :]

    def x_copy(dx, core):
        ref = xbuf.at[place]
        target = dev(zi * NX + lax.rem(xi + dx, NX), 2 * y + core)
        return remote(ref, ref, x_send.at[dx, core], x_recv.at[place], target)

    def x_arrival(k):
        return remote(xbuf.at[k], xbuf.at[k], x_send.at[0, 0], x_recv.at[k], partner)

    def to_line(act):
        act(remote(xbuf.at[place], xbuf.at[place], x_send.at[0, 0], x_recv.at[place], partner))
        for dx in range(1, NX):
            for core in range(2):
                act(x_copy(dx, core))

    @pl.when(xi < NX - 1)
    def _():
        pl.semaphore_wait(ready.at[1], 2 * (NX - 1 - xi))

    to_line(lambda copy: copy.start())
    for k in range(2 * NX):

        @pl.when(place != k)
        def _():
            x_arrival(k).wait_recv()

    def member(k, pb):
        return tuple(lanes(xbuf[k, 6 * pb + i : 6 * pb + i + 1, :]) for i in range(6))

    partial = [[member(0, pb)] for pb in range(2)]
    for k in range(1, 2 * NX):
        for pb in range(2):
            partial[pb].append(compose(member(k, pb), partial[pb][-1]))
    for pb in range(2):
        for i in range(6):
            rowtot[6 * pb + i : 6 * pb + i + 1, :] = partial[pb][-1][i][0:1, :]

    def z_copy(dz):
        target = dev(lax.rem(zi + dz, NZ) * NX + xi, m)
        return remote(rowtot, zbuf.at[dz], z_send.at[dz], z_recv.at[dz], target)

    @pl.when(zi < NZ - 1)
    def _():
        pl.semaphore_wait(ready.at[2], NZ - 1 - zi)

    for dz in range(1, NZ):

        @pl.when(zi + dz < NZ)
        def _():
            z_copy(dz).start()

    ahead = []
    for pb in range(2):
        before = identity
        for k in range(2 * NX - 1):
            before = tuple(
                jnp.where(place == k + 1, v, w) for v, w in zip(partial[pb][k], before)
            )
        ahead.append(before)

    for dz in range(1, NZ):

        @pl.when(zi >= dz)
        def _():
            z_copy(dz).wait_recv()

    current = {}
    for pb in range(2):
        state = tuple(lanes(ini[pb, k : k + 1, :]) for k in range(2))
        for dz in range(NZ - 1, 0, -1):
            mk = tuple(lanes(zbuf[dz, 6 * pb + i : 6 * pb + i + 1, :]) for i in range(6))
            after = apply_map(mk, state)
            state = tuple(jnp.where(zi >= dz, v, w) for v, w in zip(after, state))
        state = apply_map(ahead[pb], state)
        for q in range(Q):
            current[q, pb] = apply_map(tuple(seg[q, pb, i] for i in range(6)), state)
            if q < Q - 1:
                state = apply_map(chunk_total(q, pb), state)

    for duo in ((0, 1), (2, 3)):
        chains = [(q, pb) for q in duo for pb in range(2)]
        pairs = {chain: ([], []) for chain in chains}
        for j in range(SEG):
            for q, pb in chains:
                x1, x2 = current[q, pb]
                u1 = cosine[pb] * x1 - sine[pb] * x2
                u2 = sine[pb] * x1 + cosine[pb] * x2
                x1 = terms[q, j, 4 * pb] * u1 + terms[q, j, 4 * pb + 2]
                x2 = terms[q, j, 4 * pb + 1] * u2 + terms[q, j, 4 * pb + 3]
                current[q, pb] = (x1, x2)
                at = 2 * (q * CH + j)
                nst[pb, pl.ds(at, 8, stride=2 * SEG), :] = x1
                nst[pb, pl.ds(at + 1, 8, stride=2 * SEG), :] = x2
                pairs[q, pb][0].append(x1)
                pairs[q, pb][1].append(x2)
                if j % 2 == 1:
                    for k in range(2):
                        both = jnp.concatenate(pairs[q, pb][k], axis=0).astype(BF16)
                        top = (q % 2) * CH + (j - 1) * 8
                        stb[pb, q // 2, top : top + 16, k * 128 : (k + 1) * 128] = both
                    pairs[q, pb] = ([], [])

    pltpu.make_async_copy(wo.at[c], wo.at[c], wo_sem.at[0]).wait()
    wo_all = remote(wo.at[o], wo.at[o], wo_sem.at[1], wo_sem.at[2], partner)
    wo_all.wait_recv()

    def own(k, q):
        columns = 2 * k + q // 2
        h = lax.rem(q, 2)
        part = jnp.dot(stb[0, h], wo[0, columns], preferred_element_type=F32)
        return part + jnp.dot(stb[1, h], wo[1, columns], preferred_element_type=F32)

    def rs_copy(d, i):
        return remote(
            sbuf.at[d, i], rbuf.at[d, i], rs_send.at[0], rs_recv.at[d, i], (up, down)[d]
        )

    def last_copy(d, i):
        q = lax.rem(i + 2 * d, 4)
        h = lax.rem(q, 2)
        target = dev(s, 2 * ring(1 if d == 0 else -1) + q // 2)
        return remote(
            sbuf.at[d, i], fbuf.at[d, c, h], rs_send.at[0], f_recv.at[d, c, h], target
        )

    def item(d, i):
        dist = (17 - i) // 4
        return own(ring(dist) if d == 0 else ring(-dist), lax.rem(i + 2 * d, 4))

    @pl.loop(0, 4)
    def _(i):
        for d in range(2):
            sbuf[d, i] = item(d, i).astype(BF16)
            rs_copy(d, i).start()

    def home(h):
        ref = nsb.at[pl.ds(pl.multiple_of(c * 2 * HALF, 2 * HALF), 2 * HALF)]
        if h == 0:
            return pltpu.make_async_copy(nst.at[c], ref, ns_sem.at[0])
        return remote(nst.at[o], ref, ns_sem.at[1], ns_sem.at[2], partner)

    home(0).start()
    home(1).start()

    def own_copy(h):
        return remote(pbuf.at[h], obuf.at[h], o_send.at[h], o_recv.at[h], partner)

    @pl.loop(4, 10)
    def _(i):
        for d in range(2):
            mine = item(d, i)
            rs_copy(d, i - 4).wait_recv()
            sbuf[d, i] = (mine + rbuf[d, i - 4].astype(F32)).astype(BF16)
            rs_copy(d, i).start()

        @pl.when(i < 6)
        def _():
            h = i - 4
            fin[h] = own(y, 2 * c + h)
            pbuf[h] = own(y, 2 * o + h).astype(BF16)
            own_copy(h).start()

    @pl.loop(10, STEPS)
    def _(i):
        for d in range(2):
            mine = item(d, i)
            rs_copy(d, i - 4).wait_recv()
            sbuf[d, i] = (mine + rbuf[d, i - 4].astype(F32)).astype(BF16)
            last_copy(d, i).start()

    def landed(d, core, h):
        ref = fbuf.at[d, core, h]
        return remote(ref, ref, rs_send.at[0], f_recv.at[d, core, h], partner)

    for h in range(2):
        own_copy(h).wait_recv()
        for mine in (True, False):
            core = c if mine else o
            base = fin[h] if mine else obuf[h].astype(F32)
            landed(o, core, h).wait_recv()
            fin[h if mine else 2 + h] = base + fbuf[o, core, h].astype(F32)
    for h in range(2):
        for mine in (True, False):
            core = c if mine else o
            landed(c, core, h).wait_recv()
            total = fin[h if mine else 2 + h] + fbuf[c, core, h].astype(F32)
            slot = 0 if mine else 1
            for u in range(TALL // CH):
                for j in range(SEG):
                    for k in range(2):
                        top = u * CH + j * 8
                        otmp[slot, k, pl.ds(u * CH + j, 8, stride=SEG), :] = total[
                            top : top + 8, k * 128 : (k + 1) * 128
                        ]
            r = pl.ds(pl.multiple_of(core * HALF + h * TALL, TALL), TALL)
            for k in range(2):
                outb[r, k * 128 : (k + 1) * 128] = otmp[slot, k].astype(BF16)

    def sent(ref, sem):
        remote(ref, ref, sem, rs_recv.at[0, 0], partner).wait_send()

    first.wait_send()
    for i in range(4):
        small_copy(i).wait_send()
    for core in range(2):

        @pl.when(c == core)
        def _():
            guess_to(1 - core).wait_send()

    @pl.when(s < NS - 1)
    def _():
        edge(c).wait_send()

    sent(xg.at[pl.ds(0, 14)], ag_send.at[0])
    sent(wi.at[c], wi_send.at[0])
    wo_all.wait_send()
    to_line(lambda copy: copy.wait_send())
    for dz in range(1, NZ):

        @pl.when(zi + dz < NZ)
        def _():
            z_copy(dz).wait_send()

    home(0).wait()
    home(1).wait_send()
    other_half = nsb.at[pl.ds(pl.multiple_of(o * 2 * HALF, 2 * HALF), 2 * HALF)]
    remote(nst.at[o], other_half, ns_sem.at[1], ns_sem.at[2], partner).wait_recv()
    for h in range(2):
        own_copy(h).wait_send()
    sent(sbuf, rs_send.at[0])


def write_out(state, out, state_hbm, out_hbm, sem):
    copies = (
        pltpu.make_async_copy(state, state_hbm, sem.at[0]),
        pltpu.make_async_copy(out, out_hbm, sem.at[1]),
    )
    for copy in copies:
        copy.start()
    for copy in copies:
        copy.wait()


def local(inputs, guess, initial, w_in, bias, angle, strength, w_out):
    dma = pltpu.SemaphoreType.DMA
    hbm = pl.BlockSpec(memory_space=pltpu.HBM)
    vmem = pl.BlockSpec(memory_space=pltpu.VMEM)
    new_state, output = pl.pallas_call(
        kernel,
        out_shape=(
            jax.ShapeDtypeStruct((2 * ROWS, 128), F32),
            jax.ShapeDtypeStruct((ROWS, BLK), BF16),
        ),
        in_specs=[hbm] * 8,
        out_specs=(vmem, vmem),
        scratch_shapes=[
            pltpu.VMEM((16, HALF, BLK), BF16),
            pltpu.VMEM((8192, 128), BF16),
            pltpu.VMEM((2, 16, BLK, BLK), BF16),
            pltpu.VMEM((2 * BLK, 128), F32),
            pltpu.VMEM((2, 16, BLK, BLK), BF16),
            pltpu.VMEM((4, HALF, 128), F32),
            pltpu.VMEM((2, 8 + 2 * HALF, 128), F32),
            pltpu.VMEM((Q, SEG, 4, 8, 128), F32),
            pltpu.VMEM((Q, SEG, 8, 8, 128), F32),
            pltpu.VMEM((Q, 2, 12, 8, 128), F32),
            pltpu.VMEM((2 * NX, 12, 128), F32),
            pltpu.VMEM((12, 128), F32),
            pltpu.VMEM((NZ, 12, 128), F32),
            pltpu.VMEM((2, 2 * HALF, 128), F32),
            pltpu.VMEM((2, 2, TALL, BLK), BF16),
            pltpu.VMEM((2, STEPS, TALL, BLK), BF16),
            pltpu.VMEM((2, 10, TALL, BLK), BF16),
            pltpu.VMEM((2, 2, 2, TALL, BLK), BF16),
            pltpu.VMEM((2, TALL, BLK), BF16),
            pltpu.VMEM((2, TALL, BLK), BF16),
            pltpu.VMEM((4, TALL, BLK), F32),
            pltpu.VMEM((2, 2, TALL, 128), F32),
            pltpu.VMEM((2, 2, 128), F32),
            pltpu.VMEM((2, 2, 128), F32),
            pltpu.VMEM((2, 1, 128), F32),
            pltpu.VMEM((2, 1, 128), F32),
            dma((7,)),
            dma((4,)),
            dma((4,)),
            dma((2,)),
            dma((2, 3, 4)),
            dma((2, 6)),
            dma((1,)),
            dma((1,)),
            dma((16,)),
            dma((2,)),
            dma((1,)),
            dma((2,)),
            dma((3,)),
            dma((NX, 2)),
            dma((2 * NX,)),
            dma((NZ,)),
            dma((NZ,)),
            dma((3,)),
            dma((2,)),
            dma((2,)),
            dma((1,)),
            dma((2, 10)),
            dma((2, 2, 2)),
            pltpu.SemaphoreType.REGULAR((3,)),
        ],
        compiler_params=pltpu.CompilerParams(
            collective_id=0, has_side_effects=True, vmem_limit_bytes=48 * 1024 * 1024
        ),
    )(*(pltpu.with_memory_space_constraint(v, pltpu.HBM) for v in (
        inputs,
        guess.reshape(2 * ROWS, 128),
        initial,
        w_in.reshape(8192, 128),
        bias,
        angle.reshape(1, 128),
        strength.reshape(1, 128),
        w_out.reshape(BLK, 4096),
    )))
    new_state, output = pl.pallas_call(
        write_out,
        out_shape=(
            jax.ShapeDtypeStruct((2 * ROWS, 128), F32),
            jax.ShapeDtypeStruct((ROWS, BLK), BF16),
        ),
        in_specs=[pl.BlockSpec(memory_space=pl.ANY)] * 2,
        out_specs=(hbm, hbm),
        scratch_shapes=[dma((2,))],
        compiler_params=pltpu.CompilerParams(vmem_limit_bytes=4 * 1024 * 1024),
    )(new_state, output)
    return new_state.reshape(ROWS, 2, 128), output


def solution(mesh):
    placed = (
        P("seq", "mp"),
        P("seq", None, "mp"),
        P(None, "mp"),
        P(None, None, "mp"),
        P(None, "mp"),
        P("mp"),
        P("mp"),
        P(None, "mp", None),
    )
    return jax.shard_map(
        local,
        mesh=mesh,
        in_specs=placed,
        out_specs=(P("seq", None, "mp"), P("seq", "mp")),
        check_vma=False,
    )
```

time: 312 us -> 61.2 us (0.20)
  the two profiles are of different devices: /device:TPU:8 before, /device:TPU:449 now
where the time goes in v3:
time: 61.2 us; the launch traced here: 60.2 us
  Pallas kernels  59.5 us (97%)
  between operations  0.64 us (1%)
    pallas_call x1, Pallas kernels, local(): pl.pallas_call(kernel, out_shape=(jax.ShapeDtypeStruct((2 * ROWS, 128), F...  58.6 us

profile of v3, /device:TPU:449, one launch (start us, length us, event | category | flops | bytes accessed | tf_op | source)
XLA Modules:
  0.0 60.2 jit_solution(5822396132134803482)
XLA Ops:
  0.6 58.6 %shard_map.95 = (f32[1024,128]{1,0:T(8,128)S(1)}, bf16[512,256]{1,0:T(8,128)(2,1)S(1)}) custom-call(bf16[512,256]{1,0:T(8,128)(2,1)} %x_hbm.1, f32[1024,128]{1,0:T(8,128)} %bitcast.8, f32[2,128]{1,0:T(2,128)} %init_hbm.1, bf16[8192,128]{1,0:T(8,128)(2,1)} %bitcast.6, f32[2,128]{1,0:T(2,128)} %bias_hbm.1, f32[1,128]{1,0:T(1,128)} %bitcast.9, ...), custom_call_target="tpu_custom_call" | custom-call | tf_op jit(solution)/shard_map/pallas_call | solution.py:743
  59.3 0.9 %shard_map.96 = (f32[1024,128]{1,0:T(8,128)}, bf16[512,256]{1,0:T(8,128)(2,1)}) custom-call(f32[1024,128]{1,0:T(8,128)S(1)} %get-tuple-element.6.state, bf16[512,256]{1,0:T(8,128)(2,1)S(1)} %get-tuple-element.7.out), custom_call_target="tpu_custom_call" | custom-call | tf_op jit(solution)/shard_map/pallas_call | solution.py:816

commit v4 on v3

--- a/solution.py
+++ b/solution.py
@@ -20,6 +20,7 @@
 Q = 4
 CH = HALF // Q
 SEG = CH // 8
+LEAD = 1
 STEPS = 14
 
 
@@ -63,6 +64,8 @@
     rot,
     terms,
     seg,
+    hbuf,
+    ebuf,
     xbuf,
     rowtot,
     zbuf,
@@ -92,6 +95,7 @@
     e_send,
     e_recv,
     wo_sem,
+    h_sem,
     x_send,
     x_recv,
     z_send,
@@ -159,14 +163,13 @@
 
     for dx in range(1, NX):
 
-        @pl.when(xi + dx < NX)
-        def _():
-            for core in range(2):
-                greet(dev(s + dx, 2 * y + core))
+        @pl.when((xi + dx < NX) & (c == LEAD))
+        def _():
+            greet(dev(s + dx, m))
 
     for dz in range(1, NZ):
 
-        @pl.when(zi + dz < NZ)
+        @pl.when((zi + dz < NZ) & (c == LEAD))
         def _():
             greet(dev(s + dz * NX, m))
 
@@ -174,7 +177,7 @@
     def _():
         greet(dev(s + 1, 2 * y))
 
-    pl.semaphore_wait(barrier, 5 + 2 * xi + zi + 2 * (lax.min(s, 1) * o))
+    pl.semaphore_wait(barrier, 5 + (c if LEAD == 1 else o) * (xi + zi) + 2 * (lax.min(s, 1) * o))
 
     def answer(sem, target):
         pl.semaphore_signal(sem, inc=1, device_id=target, device_id_type=MESH)
@@ -220,14 +223,13 @@
 
     for dx in range(1, NX):
 
-        @pl.when(xi >= dx)
-        def _():
-            for core in range(2):
-                answer(ready.at[1], dev(s - dx, 2 * y + core))
+        @pl.when((xi >= dx) & (c == LEAD))
+        def _():
+            answer(ready.at[1], dev(s - dx, m))
 
     for dz in range(1, NZ):
 
-        @pl.when(zi >= dz)
+        @pl.when((zi >= dz) & (c == LEAD))
         def _():
             answer(ready.at[2], dev(s - dz * NX, m))
 
@@ -485,91 +487,143 @@
     def chunk_total(q, pb):
         return tuple(seg[q, pb, 6 + i] for i in range(6))
 
-    place = 2 * xi + c
+    def rows_of(ref, pb):
+        return tuple(lanes(ref[6 * pb + i : 6 * pb + i + 1, :]) for i in range(6))
+
+    def keep(ref, pb, mm):
+        for i in range(6):
+            ref[6 * pb + i : 6 * pb + i + 1, :] = mm[i][0:1, :]
+
     for pb in range(2):
         whole = chunk_total(0, pb)
         for q in range(1, Q):
             whole = compose(chunk_total(q, pb), whole)
-        for i in range(6):
-            xbuf[place, 6 * pb + i : 6 * pb + i + 1, :] = whole[i][0:1, :]
-
-    def x_copy(dx, core):
-        ref = xbuf.at[place]
-        target = dev(zi * NX + lax.rem(xi + dx, NX), 2 * y + core)
-        return remote(ref, ref, x_send.at[dx, core], x_recv.at[place], target)
+        keep(hbuf.at[c], pb, whole)
+
+    half_copy = remote(hbuf.at[1 - LEAD], hbuf.at[1 - LEAD], h_sem.at[0], h_sem.at[1], partner)
+    state_copy = remote(ebuf.at[1 - LEAD], ebuf.at[1 - LEAD], h_sem.at[2], h_sem.at[3], partner)
+
+    def x_copy(dx):
+        ref = xbuf.at[xi]
+        target = dev(zi * NX + lax.rem(xi + dx, NX), m)
+        return remote(ref, ref, x_send.at[dx], x_recv.at[xi], target)
 
     def x_arrival(k):
-        return remote(xbuf.at[k], xbuf.at[k], x_send.at[0, 0], x_recv.at[k], partner)
-
-    def to_line(act):
-        act(remote(xbuf.at[place], xbuf.at[place], x_send.at[0, 0], x_recv.at[place], partner))
-        for dx in range(1, NX):
-            for core in range(2):
-                act(x_copy(dx, core))
-
-    @pl.when(xi < NX - 1)
-    def _():
-        pl.semaphore_wait(ready.at[1], 2 * (NX - 1 - xi))
-
-    to_line(lambda copy: copy.start())
-    for k in range(2 * NX):
-
-        @pl.when(place != k)
-        def _():
-            x_arrival(k).wait_recv()
-
-    def member(k, pb):
-        return tuple(lanes(xbuf[k, 6 * pb + i : 6 * pb + i + 1, :]) for i in range(6))
-
-    partial = [[member(0, pb)] for pb in range(2)]
-    for k in range(1, 2 * NX):
-        for pb in range(2):
-            partial[pb].append(compose(member(k, pb), partial[pb][-1]))
-    for pb in range(2):
-        for i in range(6):
-            rowtot[6 * pb + i : 6 * pb + i + 1, :] = partial[pb][-1][i][0:1, :]
+        return remote(xbuf.at[k], xbuf.at[k], x_send.at[0], x_recv.at[k], partner)
 
     def z_copy(dz):
         target = dev(lax.rem(zi + dz, NZ) * NX + xi, m)
         return remote(rowtot, zbuf.at[dz], z_send.at[dz], z_recv.at[dz], target)
 
-    @pl.when(zi < NZ - 1)
+    @pl.when(c != LEAD)
     def _():
-        pl.semaphore_wait(ready.at[2], NZ - 1 - zi)
-
-    for dz in range(1, NZ):
-
-        @pl.when(zi + dz < NZ)
-        def _():
-            z_copy(dz).start()
-
-    ahead = []
-    for pb in range(2):
-        before = identity
-        for k in range(2 * NX - 1):
-            before = tuple(
-                jnp.where(place == k + 1, v, w) for v, w in zip(partial[pb][k], before)
-            )
-        ahead.append(before)
-
-    for dz in range(1, NZ):
-
-        @pl.when(zi >= dz)
-        def _():
-            z_copy(dz).wait_recv()
+        half_copy.start()
+
+    @pl.when(c == LEAD)
+    def _():
+        @pl.when(xi < NX - 1)
+        def _():
+            pl.semaphore_wait(ready.at[1], NX - 1 - xi)
+
+        @pl.when(zi < NZ - 1)
+        def _():
+            pl.semaphore_wait(ready.at[2], NZ - 1 - zi)
+
+        half_copy.wait_recv()
+        for pb in range(2):
+            keep(xbuf.at[xi], pb, compose(rows_of(hbuf.at[1], pb), rows_of(hbuf.at[0], pb)))
+        for dx in range(1, NX):
+            x_copy(dx).start()
+        for k in range(NX):
+
+            @pl.when(xi != k)
+            def _():
+                x_arrival(k).wait_recv()
+
+        partial = [[rows_of(xbuf.at[0], pb)] for pb in range(2)]
+        for k in range(1, NX):
+            for pb in range(2):
+                partial[pb].append(compose(rows_of(xbuf.at[k], pb), partial[pb][-1]))
+        for pb in range(2):
+            keep(rowtot, pb, partial[pb][-1])
+
+        for dz in range(1, NZ):
+
+            @pl.when(zi + dz < NZ)
+            def _():
+                z_copy(dz).start()
+
+        ahead = []
+        for pb in range(2):
+            before = identity
+            for k in range(NX - 1):
+                before = tuple(
+                    jnp.where(xi == k + 1, v, w) for v, w in zip(partial[pb][k], before)
+                )
+            ahead.append(before)
+
+        for dz in range(1, NZ):
+
+            @pl.when(zi >= dz)
+            def _():
+                z_copy(dz).wait_recv()
+
+        for pb in range(2):
+            state = tuple(lanes(ini[pb, k : k + 1, :]) for k in range(2))
+            for dz in range(NZ - 1, 0, -1):
+                after = apply_map(rows_of(zbuf.at[dz], pb), state)
+                state = tuple(jnp.where(zi >= dz, v, w) for v, w in zip(after, state))
+            state = apply_map(ahead[pb], state)
+            later = apply_map(rows_of(hbuf.at[0], pb), state)
+            for k in range(2):
+                at = 2 * pb + k
+                ebuf[0, at : at + 1, :] = state[k][0:1, :]
+                ebuf[1, at : at + 1, :] = later[k][0:1, :]
+        state_copy.start()
+
+    @pl.when(c != LEAD)
+    def _():
+        state_copy.wait_recv()
 
     current = {}
     for pb in range(2):
-        state = tuple(lanes(ini[pb, k : k + 1, :]) for k in range(2))
-        for dz in range(NZ - 1, 0, -1):
-            mk = tuple(lanes(zbuf[dz, 6 * pb + i : 6 * pb + i + 1, :]) for i in range(6))
-            after = apply_map(mk, state)
-            state = tuple(jnp.where(zi >= dz, v, w) for v, w in zip(after, state))
-        state = apply_map(ahead[pb], state)
+        state = tuple(lanes(ebuf[c, 2 * pb + k : 2 * pb + k + 1, :]) for k in range(2))
         for q in range(Q):
             current[q, pb] = apply_map(tuple(seg[q, pb, i] for i in range(6)), state)
             if q < Q - 1:
                 state = apply_map(chunk_total(q, pb), state)
+
+    pltpu.make_async_copy(wo.at[c], wo.at[c], wo_sem.at[0]).wait()
+    wo_all = remote(wo.at[o], wo.at[o], wo_sem.at[1], wo_sem.at[2], partner)
+    wo_all.wait_recv()
+
+    def own(k, q):
+        columns = 2 * k + q // 2
+        h = lax.rem(q, 2)
+        part = jnp.dot(stb[0, h], wo[0, columns], preferred_element_type=F32)
+        return part + jnp.dot(stb[1, h], wo[1, columns], preferred_element_type=F32)
+
+    def rs_copy(d, i):
+        return remote(
+            sbuf.at[d, i], rbuf.at[d, i], rs_send.at[0], rs_recv.at[d, i], (up, down)[d]
+        )
+
+    def last_copy(d, i):
+        q = lax.rem(i + 2 * d, 4)
+        h = lax.rem(q, 2)
+        target = dev(s, 2 * ring(1 if d == 0 else -1) + q // 2)
+        return remote(
+            sbuf.at[d, i], fbuf.at[d, c, h], rs_send.at[0], f_recv.at[d, c, h], target
+        )
+
+    def item(d, i):
+        dist = (17 - i) // 4
+        return own(ring(dist) if d == 0 else ring(-dist), lax.rem(i + 2 * d, 4))
+
+    def begin(i):
+        for d in range(2):
+            sbuf[d, i] = item(d, i).astype(BF16)
+            rs_copy(d, i).start()
 
     for duo in ((0, 1), (2, 3)):
         chains = [(q, pb) for q in duo for pb in range(2)]
@@ -594,38 +648,12 @@
                         stb[pb, q // 2, top : top + 16, k * 128 : (k + 1) * 128] = both
                     pairs[q, pb] = ([], [])
 
-    pltpu.make_async_copy(wo.at[c], wo.at[c], wo_sem.at[0]).wait()
-    wo_all = remote(wo.at[o], wo.at[o], wo_sem.at[1], wo_sem.at[2], partner)
-    wo_all.wait_recv()
-
-    def own(k, q):
-        columns = 2 * k + q // 2
-        h = lax.rem(q, 2)
-        part = jnp.dot(stb[0, h], wo[0, columns], preferred_element_type=F32)
-        return part + jnp.dot(stb[1, h], wo[1, columns], preferred_element_type=F32)
-
-    def rs_copy(d, i):
-        return remote(
-            sbuf.at[d, i], rbuf.at[d, i], rs_send.at[0], rs_recv.at[d, i], (up, down)[d]
-        )
-
-    def last_copy(d, i):
-        q = lax.rem(i + 2 * d, 4)
-        h = lax.rem(q, 2)
-        target = dev(s, 2 * ring(1 if d == 0 else -1) + q // 2)
-        return remote(
-            sbuf.at[d, i], fbuf.at[d, c, h], rs_send.at[0], f_recv.at[d, c, h], target
-        )
-
-    def item(d, i):
-        dist = (17 - i) // 4
-        return own(ring(dist) if d == 0 else ring(-dist), lax.rem(i + 2 * d, 4))
-
-    @pl.loop(0, 4)
+        if duo == (0, 1):
+            begin(0)
+
+    @pl.loop(1, 4)
     def _(i):
-        for d in range(2):
-            sbuf[d, i] = item(d, i).astype(BF16)
-            rs_copy(d, i).start()
+        begin(i)
 
     def home(h):
         ref = nsb.at[pl.ds(pl.multiple_of(c * 2 * HALF, 2 * HALF), 2 * HALF)]
@@ -709,12 +737,21 @@
     sent(xg.at[pl.ds(0, 14)], ag_send.at[0])
     sent(wi.at[c], wi_send.at[0])
     wo_all.wait_send()
-    to_line(lambda copy: copy.wait_send())
-    for dz in range(1, NZ):
-
-        @pl.when(zi + dz < NZ)
-        def _():
-            z_copy(dz).wait_send()
+
+    @pl.when(c != LEAD)
+    def _():
+        half_copy.wait_send()
+
+    @pl.when(c == LEAD)
+    def _():
+        state_copy.wait_send()
+        for dx in range(1, NX):
+            x_copy(dx).wait_send()
+        for dz in range(1, NZ):
+
+            @pl.when(zi + dz < NZ)
+            def _():
+                z_copy(dz).wait_send()
 
     home(0).wait()
     home(1).wait_send()
@@ -759,7 +796,9 @@
             pltpu.VMEM((Q, SEG, 4, 8, 128), F32),
             pltpu.VMEM((Q, SEG, 8, 8, 128), F32),
             pltpu.VMEM((Q, 2, 12, 8, 128), F32),
-            pltpu.VMEM((2 * NX, 12, 128), F32),
+            pltpu.VMEM((2, 12, 128), F32),
+            pltpu.VMEM((2, 8, 128), F32),
+            pltpu.VMEM((NX, 12, 128), F32),
             pltpu.VMEM((12, 128), F32),
             pltpu.VMEM((NZ, 12, 128), F32),
             pltpu.VMEM((2, 2 * HALF, 128), F32),
@@ -788,8 +827,9 @@
             dma((1,)),
             dma((2,)),
             dma((3,)),
-            dma((NX, 2)),
-            dma((2 * NX,)),
+            dma((4,)),
+            dma((NX,)),
+            dma((NX,)),
             dma((NZ,)),
             dma((NZ,)),
             dma((3,)),

time: 61.2 us -> 60.2 us (0.984); the launches traced: 60.2 us -> 59.8 us
  no operation moved by 1% of the time
where the time goes in v4:
time: 60.2 us; the launch traced here: 59.8 us
  Pallas kernels  59.2 us (98%)
  between operations  0.64 us (1%)
    pallas_call x1, Pallas kernels, local(): pl.pallas_call(kernel, out_shape=(jax.ShapeDtypeStruct((2 * ROWS, 128), F...  58.3 us

profile of v4, /device:TPU:449, one launch (start us, length us, event | category | flops | bytes accessed | tf_op | source)
XLA Modules:
  0.0 59.8 jit_solution(17022414631307230687)
XLA Ops:
  0.6 58.3 %shard_map.95 = (f32[1024,128]{1,0:T(8,128)S(1)}, bf16[512,256]{1,0:T(8,128)(2,1)S(1)}) custom-call(bf16[512,256]{1,0:T(8,128)(2,1)} %x_hbm.1, f32[1024,128]{1,0:T(8,128)} %bitcast.8, f32[2,128]{1,0:T(2,128)} %init_hbm.1, bf16[8192,128]{1,0:T(8,128)(2,1)} %bitcast.6, f32[2,128]{1,0:T(2,128)} %bias_hbm.1, f32[1,128]{1,0:T(1,128)} %bitcast.9, ...), custom_call_target="tpu_custom_call" | custom-call | tf_op jit(solution)/shard_map/pallas_call | solution.py:780
  58.9 0.9 %shard_map.96 = (f32[1024,128]{1,0:T(8,128)}, bf16[512,256]{1,0:T(8,128)(2,1)}) custom-call(f32[1024,128]{1,0:T(8,128)S(1)} %get-tuple-element.6.state, bf16[512,256]{1,0:T(8,128)(2,1)S(1)} %get-tuple-element.7.out), custom_call_target="tpu_custom_call" | custom-call | tf_op jit(solution)/shard_map/pallas_call | solution.py:856

commit v5 on v4

--- a/solution.py
+++ b/solution.py
@@ -260,7 +260,10 @@
             partner,
         )
 
-    first_recv = first.wait_recv
+    first.wait_recv()
+    for a in range(2, 4):
+        for d in range(2):
+            ici(y, a, 0, d).start()
     w_copy.wait()
 
     def prepare(b):
@@ -273,10 +276,6 @@
         return remote(wi.at[pb, b], wi.at[pb, b], wi_send.at[0], wi_recv.at[b], partner)
 
     prepare(m)
-    first_recv()
-    for a in range(2, 4):
-        for d in range(2):
-            ici(y, a, 0, d).start()
     prepare(other)
 
     for core in range(2):
@@ -532,7 +531,7 @@
         half_copy.wait_recv()
         for pb in range(2):
             keep(xbuf.at[xi], pb, compose(rows_of(hbuf.at[1], pb), rows_of(hbuf.at[0], pb)))
-        for dx in range(1, NX):
+        for dx in (2, 1, 3):
             x_copy(dx).start()
         for k in range(NX):
 
@@ -547,7 +546,7 @@
         for pb in range(2):
             keep(rowtot, pb, partial[pb][-1])
 
-        for dz in range(1, NZ):
+        for dz in (4, 3, 5, 2, 6, 1, 7):
 
             @pl.when(zi + dz < NZ)
             def _():

time: 60.2 us -> 60.4 us (level)
  no operation moved by 1% of the time
where the time goes in v5:
time: 60.4 us; the launch traced here: 59.7 us
  Pallas kernels  59 us (98%)
  between operations  0.64 us (1%)
    pallas_call x1, Pallas kernels, local(): pl.pallas_call(kernel, out_shape=(jax.ShapeDtypeStruct((2 * ROWS, 128), F...  58.1 us

profile of v5, /device:TPU:449, one launch (start us, length us, event | category | flops | bytes accessed | tf_op | source)
XLA Modules:
  0.0 59.7 jit_solution(1965344951930719184)
XLA Ops:
  0.6 58.1 %shard_map.95 = (f32[1024,128]{1,0:T(8,128)S(1)}, bf16[512,256]{1,0:T(8,128)(2,1)S(1)}) custom-call(bf16[512,256]{1,0:T(8,128)(2,1)} %x_hbm.1, f32[1024,128]{1,0:T(8,128)} %bitcast.8, f32[2,128]{1,0:T(2,128)} %init_hbm.1, bf16[8192,128]{1,0:T(8,128)(2,1)} %bitcast.6, f32[2,128]{1,0:T(2,128)} %bias_hbm.1, f32[1,128]{1,0:T(1,128)} %bitcast.9, ...), custom_call_target="tpu_custom_call" | custom-call | tf_op jit(solution)/shard_map/pallas_call | solution.py:779
  58.8 0.9 %shard_map.96 = (f32[1024,128]{1,0:T(8,128)}, bf16[512,256]{1,0:T(8,128)(2,1)}) custom-call(f32[1024,128]{1,0:T(8,128)S(1)} %get-tuple-element.6.state, bf16[512,256]{1,0:T(8,128)(2,1)S(1)} %get-tuple-element.7.out), custom_call_target="tpu_custom_call" | custom-call | tf_op jit(solution)/shard_map/pallas_call | solution.py:855
